TPU v7x, 256 devices: a whole 4x4x8 slice. The times are simulated.
256 devices in a mesh: row: 8 (over x, core), col: 8 (over z), fit: 4 (over y).
Axes of the slice: x: 4, y: 4, z: 8, core: 2. Of those that a mesh axis runs over, the one named last changes fastest.
Arguments:
- orbital_ints: bfloat16 [128, 40, 2560], P(('row', 'col'), None, 'fit'), may hold values from -0.83984375 to 0.83984375
- occ_energy: float32 [128], P(('row', 'col')), may hold values from -1.2 to -0.3
- pair_row: int32 [8192], P(('row', 'col')), may hold values from 0 to 15
- pair_col: int32 [8192], P(('row', 'col')), may hold values from 0 to 15
- virt_energy: float32 [40, 8192], P(None, ('row', 'col')), may hold values from 0.5 to 3
- amplitudes: float32 [40, 40, 8192], P(None, None, ('row', 'col')), may hold values from -1.8 to 1.8
- intersections: bfloat16 [40, 40, 16, 8192], P(None, None, 'fit', ('row', 'col')), may hold values from -1 to 1
- coupling_fock: float32 [16, 8192], P('fit', ('row', 'col')), may hold values from -0.25 to 0.25
- partner_owner: int32 [4, 8192, 4], P('fit', ('row', 'col')), may hold values from 0 to 63, all different within a row; in each aligned block of 128 rows (0 to 127, 128 to 255, ..., all dimensions but the last counted through in order) at most 16 rows name the same one
- partner_slot: int32 [4, 8192, 4], P('fit', ('row', 'col')), may hold values from 0 to 127
Outputs:
- new_amplitudes: float32 [40, 40, 8192], P(None, None, ('row', 'col'))
- residual: float32 [40, 40, 8192], P(None, None, ('row', 'col'))
Inputs may be any that keep to these rules, and one draw needn't show every extreme that they name: `partner_owner`: the 4 owners of one pair in one fit index differ; among the pairs of one group in one fit index (aligned blocks of 128 rows) no owner is named more than 16 times, a bound that some block reaches.
All inputs are finite; a program needn't handle non-finite values.
Results may differ from a plain program's by a relative error of at most 0.014.
Values may be sent and summed in bfloat16 or wider, within the bound.
No kernel may reach another device: no remote copies, remote signals or barrier semaphores. Data moves between devices by JAX's collectives and lax.ppermute only.
A program may use at most 128 MiB of HBM per device.

v0:
```python
import math

import jax
import jax.numpy as jnp
from jax import lax
from jax.sharding import PartitionSpec as P

ITERS = 2


def in_order(tiles, dim):
    tiles = jnp.moveaxis(tiles, 0, dim)
    lengths = tiles.shape
    return tiles.reshape(*lengths[:dim], lengths[dim] * lengths[dim + 1], *lengths[dim + 2 :])


def from_everyone(x, axis):
    copies = jnp.broadcast_to(x, (lax.axis_size(axis), *x.shape))
    return lax.all_to_all(copies, axis, split_axis=0, concat_axis=0, tiled=True)


def gathered_copies(x, axis, dim):
    return in_order(from_everyone(x, axis), dim)


def taken_together(x, axis):
    return from_everyone(x, axis).astype(jnp.float32).sum(axis=0)


def on_device(
    orbital_ints,
    occ_energy,
    pair_row,
    pair_col,
    virt_energy,
    amplitudes,
    intersections,
    coupling_fock,
    partner_owner,
    partner_slot,
):
    row_count = lax.axis_size("row")
    col_count = lax.axis_size("col")
    group_count = row_count * col_count
    tile_size = amplitudes.shape[0]
    pair_count = amplitudes.shape[2]
    link_count = partner_owner.shape[2]
    capacity = 2 * pair_count * link_count // group_count
    row_ints, row_energy = (
        gathered_copies(orbital_ints, "col", 0),
        gathered_copies(occ_energy.astype(jnp.bfloat16), "col", 0).astype(occ_energy.dtype),
    )
    col_ints, col_energy = (
        gathered_copies(orbital_ints, "row", 0),
        gathered_copies(occ_energy.astype(jnp.bfloat16), "row", 0).astype(occ_energy.dtype),
    )
    block_width = math.gcd(pair_count, 128)
    blocks = pair_count // block_width

    def kernel_block(indices):
        first_ints = jnp.take(row_ints, indices[0], axis=0)
        second_ints = jnp.take(col_ints, indices[1], axis=0)
        return jnp.einsum(
            "pax,pbx->abp", first_ints, second_ints, preferred_element_type=jnp.float32
        )

    stacked = lax.map(
        kernel_block, (pair_row.reshape(blocks, block_width), pair_col.reshape(blocks, block_width))
    )
    partial_kernel = jnp.transpose(stacked, (1, 2, 0, 3)).reshape(tile_size, tile_size, pair_count)
    denominator = (
        virt_energy[:, None, :]
        + virt_energy[None, :, :]
        - (row_energy[pair_row] + col_energy[pair_col])[None, None, :]
    )
    owners = partner_owner[0].T.reshape(-1)
    owner_slots = partner_slot[0].T.reshape(-1)
    onehot = (owners[:, None] == jnp.arange(group_count, dtype=jnp.int32)[None, :]).astype(
        jnp.int32
    )
    position = jnp.sum((jnp.cumsum(onehot, axis=0) - 1) * onehot, axis=1)
    target = owners * capacity + position
    requests = jnp.zeros((group_count * capacity,), jnp.int32).at[target].set(owner_slots)
    incoming = lax.all_to_all(requests, ("row", "col"), split_axis=0, concat_axis=0, tiled=True)
    kernel = taken_together(partial_kernel.astype(jnp.bfloat16), "fit").astype(jnp.float32)
    current = amplitudes
    residual = amplitudes
    for turn_index in range(ITERS):
        sent_tiles = current.astype(jnp.bfloat16)
        outgoing = jnp.take(sent_tiles, incoming, axis=2)
        returned = lax.all_to_all(outgoing, ("row", "col"), split_axis=2, concat_axis=2, tiled=True)
        coupled_tiles = jnp.take(returned, target, axis=2).reshape(
            tile_size, tile_size, link_count, pair_count
        )
        half_product = jnp.einsum(
            "abcp,bdcp->adcp", intersections, coupled_tiles, preferred_element_type=jnp.float32
        ).astype(jnp.bfloat16)
        coupled = jnp.einsum(
            "adcp,edcp->aecp", half_product, intersections, preferred_element_type=jnp.float32
        )
        coupling = jnp.sum(coupled * coupling_fock[None, None, :, :], axis=2)
        residual = (
            kernel
            + denominator * current
            - taken_together(coupling.astype(jnp.bfloat16), "fit").astype(jnp.float32)
        )
        current = current - residual / denominator
    return (current, residual)


def solution(mesh):
    placed = (
        P(("row", "col"), None, "fit"),
        P(("row", "col")),
        P(("row", "col")),
        P(("row", "col")),
        P(None, ("row", "col")),
        P(None, None, ("row", "col")),
        P(None, None, "fit", ("row", "col")),
        P("fit", ("row", "col")),
        P("fit", ("row", "col"), None),
        P("fit", ("row", "col"), None),
    )
    return jax.shard_map(
        on_device,
        mesh=mesh,
        in_specs=placed,
        out_specs=(P(None, None, ("row", "col")), P(None, None, ("row", "col"))),
        check_vma=False,
    )
```

profile of v0, /device:TPU:32, one launch (start us, length us, event | category | flops | bytes accessed | tf_op | source)
XLA Modules:
  0.0 484.8 jit_solution(8918108452195344306)
XLA Ops:
  4.3 2.6 scatter_custom_fusion
  7.0 20.0 %all_to_all.59 = s32[64,16,1]{1,2,0:T(1,128)S(1)} all-to-all(s32[64,16,1]{1,2,0:T(1,128)S(1)} %bitcast.120), channel_id=1, replica_groups=mesh['row'=8,'col'=8,'fit'=4] {'row','col'}, dimensions={0} | all-to-all | bytes 8192 | tf_op jit(solution)/shard_map/all_to_all | solution.py:84
  28.9 3.5 all-to-all-start
  36.4 9.4 %all-to-all-done = bf16[8,2,40,640]{3,2,1,0:T(8,128)(2,1)S(1)} async-done(((bf16[8,2,40,640]{3,2,1,0:T(8,128)(2,1)}), bf16[8,2,40,640]{3,2,1,0:T(8,128)(2,1)S(1)}, u32[]{:S(2)}, u32[]{:S(2)}) %all-to-all-start) | async-done | bytes 819232 | tf_op jit(solution)/shard_map/all_to_all | solution.py:19
  45.8 4.9 %all-to-all-start.1 = ((bf16[8,2,40,640]{3,2,1,0:T(8,128)(2,1)}), bf16[8,2,40,640]{3,2,1,0:T(8,128)(2,1)S(1)}, u32[]{:S(2)}, u32[]{:S(2)}) async-start(bf16[8,2,40,640]{3,2,1,0:T(8,128)(2,1)} %broadcast_in_dim.64), calls=%async_computation.1 | async-start | bytes 1638400 | tf_op jit(solution)/shard_map/all_to_all | solution.py:19
  50.7 11.1 %gather_fusion.2 = bf16[1024,40,40]{2,1,0:T(8,128)(2,1)} fusion(bf16[40,40,128]{1,0,2:T(8,128)(2,1)S(1)} %copy.99, s32[1024]{0:T(1024)S(1)} %fusion.33), kind=kCustom, calls=%fused_computation.1.clone | custom fusion | bytes 6557696 | tf_op jit(solution)/shard_map/jit(_take)/gather | solution.py:90
  61.8 11.5 %fusion.41 = bf16[1024,40,40]{2,1,0:T(8,128)(2,1)} fusion(bf16[1024,40,40]{2,1,0:T(8,128)(2,1)} %gather_fusion.2, pred[1024]{0:T(1024)(128)(4,1)S(1)} %compare_and_fusion), kind=kLoop, calls=%fused_computation.99 | loop fusion | flops 1638400 | bytes 6554624
  73.3 21.6 %reshape.269 = bf16[64,2,12800]{2,1,0:T(2,128)(2,1)} reshape(bf16[1024,40,40]{2,1,0:T(8,128)(2,1)} %fusion.41) | data formatting | bytes 6553600
  94.9 9.0 %all-to-all-start.6 = ((bf16[64,2,12800]{2,1,0:T(2,128)(2,1)}), bf16[64,2,12800]{2,1,0:T(2,128)(2,1)}, u32[]{:S(2)}, u32[]{:S(2)}) async-start(bf16[64,2,12800]{2,1,0:T(2,128)(2,1)} %reshape.269), calls=%async_computation.6 | async-start | bytes 6553600 | tf_op jit(solution)/shard_map/all_to_all | solution.py:91
  104.0 4.7 copy.101
  108.8 4.1 gather_fusion
  112.9 4.1 gather_fusion.1
  117.0 7.2 %fusion.25 = bf16[40,40,128]{0,1,2:T(8,128)(2,1)S(1)} fusion(bf16[128,40,640]{2,1,0:T(8,128)(2,1)} %gather_fusion.1, pred[128]{0:T(512)(128)(4,1)S(1)} %get-tuple-element.69, bf16[128,40,640]{2,1,0:T(8,128)(2,1)} %gather_fusion, pred[128]{0:T(512)(128)(4,1)S(1)} %get-tuple-element.70), kind=kOutput, calls=%fused_computation.31 | convolution fusion | flops 268902400 | bytes 13517056 | tf_op jit(solution)/shard_map/while/body/eval_jaxpr/pax,pbx->abp/dot_general | solution.py:63
  125.6 54.6 %all-to-all-done.6 = bf16[64,2,12800]{2,1,0:T(2,128)(2,1)} async-done(((bf16[64,2,12800]{2,1,0:T(2,128)(2,1)}), bf16[64,2,12800]{2,1,0:T(2,128)(2,1)}, u32[]{:S(2)}, u32[]{:S(2)}) %all-to-all-start.6) | async-done | bytes 3276832 | tf_op jit(solution)/shard_map/all_to_all | solution.py:91
  180.8 4.2 all-to-all-start.4
  184.9 22.6 %reshape.270 = bf16[1024,40,40]{2,1,0:T(8,128)(2,1)} reshape(bf16[64,2,12800]{2,1,0:T(2,128)(2,1)} %all-to-all-done.6) | data formatting | bytes 6553600
  207.5 3.3 all-to-all-start.3
  210.8 7.9 %gather_fusion.3 = bf16[512,40,40]{2,1,0:T(8,128)(2,1)} fusion(bf16[40,40,1024]{1,0,2:T(8,128)(2,1)} %bitcast.114, s32[1024]{0:T(1024)S(1)} %pad_clamp_fusion), kind=kCustom, calls=%fused_computation.2.clone | custom fusion | bytes 3278848 | tf_op jit(solution)/shard_map/jit(_take)/gather | solution.py:92
  220.0 4.7 all-to-all-start.2
  224.7 6.7 %broadcast_select_fusion.1 = bf16[512,40,40]{2,1,0:T(8,128)(2,1)} fusion(bf16[512,40,40]{2,1,0:T(8,128)(2,1)} %gather_fusion.3, pred[512]{0:T(512)(128)(4,1)S(1)} %get-tuple-element.35), kind=kLoop, calls=%fused_computation.23 | loop fusion | flops 819200 | bytes 3277312 | tf_op jit(solution)/shard_map/jit(_take)/select_n | solution.py:92
  231.4 10.7 %multiply_reduce_fusion.1 = bf16[128,40,40]{2,1,0:T(8,128)(2,1)} fusion(f32[4,128]{1,0:T(4,128)S(1)} %copy-done.9, bf16[40,40,4,128]{1,0,3,2:T(8,128)(2,1)} %copy.101, bf16[40,40,4,128]{1,0,3,2:T(8,128)(2,1)} %bitcast.117), kind=kOutput, calls=%fused_computation.10 | convolution fusion | flops 133324800 | bytes 3688448 | tf_op jit(solution)/shard_map/adcp,edcp->aecp/dot_general | solution.py:98
  248.1 4.3 all-to-all-start.7
  254.1 19.9 %fusion.36 = f32[128]{0:T(128)S(1)} fusion(f32[]{:T(128)} %bitcast.19, f32[]{:T(128)} %bitcast.20, f32[]{:T(128)} %bitcast.21, f32[]{:T(128)} %bitcast.22, f32[]{:T(128)} %bitcast.23, f32[]{:T(128)} %bitcast.24, f32[]{:T(128)} %bitcast.25, f32[]{:T(128)} %bitcast.26, f32[]{:T(128)} %bitcast.27, f32[]{:T(128)} %bitcast.28, f32[]{:T(128)} %bitcast.29, ...), kind=kLoop, calls=%fused_computation.94 | loop fusion | flops 8576 | bytes 1664 | tf_op jit(solution)/shard_map/add | solution.py:74
  278.9 11.1 %gather_fusion.4 = bf16[1024,40,40]{2,1,0:T(8,128)(2,1)} fusion(bf16[40,40,128]{1,0,2:T(8,128)(2,1)S(1)} %copy.105, s32[1024]{0:T(1024)S(1)} %fusion.33), kind=kCustom, calls=%fused_computation.4.clone | custom fusion | bytes 6557696 | tf_op jit(solution)/shard_map/jit(_take)/gather | solution.py:90
  290.0 11.5 %fusion.42 = bf16[1024,40,40]{2,1,0:T(8,128)(2,1)} fusion(bf16[1024,40,40]{2,1,0:T(8,128)(2,1)} %gather_fusion.4, pred[1024]{0:T(1024)(128)(4,1)S(1)} %compare_and_fusion), kind=kLoop, calls=%fused_computation.100 | loop fusion | flops 1638400 | bytes 6554624
  301.4 20.8 %reshape.271 = bf16[64,2,12800]{2,1,0:T(2,128)(2,1)S(1)} reshape(bf16[1024,40,40]{2,1,0:T(8,128)(2,1)} %fusion.42) | data formatting | bytes 6553600
  322.2 86.4 %all_to_all.60 = bf16[64,2,12800]{2,1,0:T(2,128)(2,1)} all-to-all(bf16[64,2,12800]{2,1,0:T(2,128)(2,1)S(1)} %reshape.271), channel_id=1, replica_groups=mesh['row'=8,'col'=8,'fit'=4] {'row','col'}, dimensions={0} | all-to-all | bytes 6553600 | tf_op jit(solution)/shard_map/all_to_all | solution.py:91
  408.6 22.6 %reshape.272 = bf16[1024,40,40]{2,1,0:T(8,128)(2,1)} reshape(bf16[64,2,12800]{2,1,0:T(2,128)(2,1)} %all_to_all.60) | data formatting | bytes 6553600
  431.2 7.9 %gather_fusion.5 = bf16[512,40,40]{2,1,0:T(8,128)(2,1)} fusion(bf16[40,40,1024]{1,0,2:T(8,128)(2,1)} %bitcast.115, s32[1024]{0:T(1024)S(1)} %pad_clamp_fusion), kind=kCustom, calls=%fused_computation.5.clone | custom fusion | bytes 3278848 | tf_op jit(solution)/shard_map/jit(_take)/gather | solution.py:92
  439.0 6.7 %broadcast_select_fusion = bf16[512,40,40]{2,1,0:T(8,128)(2,1)} fusion(bf16[512,40,40]{2,1,0:T(8,128)(2,1)} %gather_fusion.5, pred[512]{0:T(512)(128)(4,1)S(1)} %get-tuple-element.35), kind=kLoop, calls=%fused_computation.22 | loop fusion | flops 819200 | bytes 3277312 | tf_op jit(solution)/shard_map/jit(_take)/select_n | solution.py:92
  445.7 9.7 %multiply_reduce_fusion = bf16[128,40,40]{2,1,0:T(8,128)(2,1)S(1)} fusion(f32[4,128]{1,0:T(4,128)S(1)} %copy-done.9, bf16[40,40,4,128]{1,0,3,2:T(8,128)(2,1)} %copy.101, bf16[40,40,4,128]{1,0,3,2:T(8,128)(2,1)} %bitcast.116), kind=kOutput, calls=%fused_computation.9 | convolution fusion | flops 133324800 | bytes 3688448 | tf_op jit(solution)/shard_map/adcp,edcp->aecp/dot_general | solution.py:98
  457.1 25.6 %all_to_all.61 = bf16[4,40,40,128]{3,2,1,0:T(8,128)(2,1)S(1)} all-to-all(bf16[4,40,40,128]{3,2,1,0:T(8,128)(2,1)S(1)} %broadcast_in_dim.71), channel_id=1, replica_groups=mesh['row'=8,'col'=8,'fit'=4] {'fit'}, dimensions={0} | all-to-all | bytes 3276800 | tf_op jit(solution)/shard_map/all_to_all | solution.py:19
  (71 shorter events, 28.8 us)
Async XLA Ops:
  28.9 17.0 %all-to-all-start = ((bf16[8,2,40,640]{3,2,1,0:T(8,128)(2,1)}), bf16[8,2,40,640]{3,2,1,0:T(8,128)(2,1)S(1)}, u32[]{:S(2)}, u32[]{:S(2)}) async-start(bf16[8,2,40,640]{3,2,1,0:T(8,128)(2,1)} %broadcast_in_dim.64), calls=%async_computation | async-start | bytes 1638400 | tf_op jit(solution)/shard_map/all_to_all | solution.py:19
  45.8 49.1 %all-to-all-start.1 = ((bf16[8,2,40,640]{3,2,1,0:T(8,128)(2,1)}), bf16[8,2,40,640]{3,2,1,0:T(8,128)(2,1)S(1)}, u32[]{:S(2)}, u32[]{:S(2)}) async-start(bf16[8,2,40,640]{3,2,1,0:T(8,128)(2,1)} %broadcast_in_dim.64), calls=%async_computation.1 | async-start | bytes 1638400 | tf_op jit(solution)/shard_map/all_to_all | solution.py:19
  94.9 9.1 %copy-start.10 = (f32[2]{0:T(128)S(1)}, f32[2]{0:T(128)}, u32[]{:S(2)}) copy-start(f32[2]{0:T(128)} %param.17) | copy-start | bytes 28
  94.9 9.1 %copy-start.4 = (bf16[40,40,4,128]{3,2,1,0:T(4,128)(2,1)S(1)}, bf16[40,40,4,128]{3,2,1,0:T(4,128)(2,1)}, u32[]{:S(2)}) copy-start(bf16[40,40,4,128]{3,2,1,0:T(4,128)(2,1)} %param.22) | copy-start | bytes 4915204
  94.9 13.8 %copy-start.8 = (s32[128]{0:T(128)S(1)}, s32[128]{0:T(128)}, u32[]{:S(2)}) copy-start(s32[128]{0:T(128)} %param.19) | copy-start | bytes 1540
  94.9 13.8 %copy-start.7 = (s32[128]{0:T(128)S(1)}, s32[128]{0:T(128)}, u32[]{:S(2)}) copy-start(s32[128]{0:T(128)} %param.18) | copy-start | bytes 1540
  94.9 13.9 %copy-start.6 = (s32[1,128,4]{1,2,0:T(4,128)S(1)}, s32[1,128,4]{1,2,0:T(4,128)}, u32[]{:S(2)}) copy-start(s32[1,128,4]{1,2,0:T(4,128)} %param.24) | copy-start | bytes 6148
  94.9 85.3 %all-to-all-start.6 = ((bf16[64,2,12800]{2,1,0:T(2,128)(2,1)}), bf16[64,2,12800]{2,1,0:T(2,128)(2,1)}, u32[]{:S(2)}, u32[]{:S(2)}) async-start(bf16[64,2,12800]{2,1,0:T(2,128)(2,1)} %reshape.269), calls=%async_computation.6 | async-start | bytes 6553600 | tf_op jit(solution)/shard_map/all_to_all | solution.py:91
  180.8 26.7 %all-to-all-start.4 = ((bf16[8,1,2]{2,1,0:T(2,128)(2,1)}), bf16[8,1,2]{2,1,0:T(2,128)(2,1)S(1)}, u32[]{:S(2)}, u32[]{:S(2)}) async-start(bf16[8,1,2]{2,1,0:T(2,128)(2,1)} %broadcast_in_dim.66), calls=%async_computation.4 | async-start | bytes 8192 | tf_op jit(solution)/shard_map/all_to_all | solution.py:19
  207.5 11.2 %all-to-all-start.3 = ((bf16[8,1,2]{2,1,0:T(2,128)(2,1)}), bf16[8,1,2]{2,1,0:T(2,128)(2,1)S(1)}, u32[]{:S(2)}, u32[]{:S(2)}) async-start(bf16[8,1,2]{2,1,0:T(2,128)(2,1)} %broadcast_in_dim.66), calls=%async_computation.3 | async-start | bytes 8192 | tf_op jit(solution)/shard_map/all_to_all | solution.py:19
  220.0 26.7 %all-to-all-start.2 = ((bf16[4,40,40,128]{3,2,1,0:T(8,128)(2,1)}), bf16[4,40,40,128]{3,2,1,0:T(8,128)(2,1)S(1)}, u32[]{:S(2)}, u32[]{:S(2)}) async-start(bf16[4,40,40,128]{3,2,1,0:T(8,128)(2,1)} %broadcast_in_dim.65), calls=%async_computation.2 | async-start | bytes 3276800 | tf_op jit(solution)/shard_map/all_to_all | solution.py:19
  224.7 6.7 %copy-start.9 = (f32[4,128]{1,0:T(4,128)S(1)}, f32[4,128]{1,0:T(4,128)}, u32[]{:S(2)}) copy-start(f32[4,128]{1,0:T(4,128)} %param.23) | copy-start | bytes 6148
  244.5 31.8 %copy-start.2 = (f32[40,40,128]{2,1,0:T(8,128)S(1)}, f32[40,40,128]{2,1,0:T(8,128)}, u32[]{:S(2)}) copy-start(f32[40,40,128]{2,1,0:T(8,128)} %param.21) | copy-start | bytes 2457604
  244.5 31.7 %copy-start.5 = (f32[40,128]{1,0:T(8,128)S(1)}, f32[40,128]{1,0:T(8,128)}, u32[]{:S(2)}) copy-start(f32[40,128]{1,0:T(8,128)} %param.20) | copy-start | bytes 61444
  248.1 26.1 %all-to-all-start.7 = ((bf16[4,40,40,128]{3,2,1,0:T(8,128)(2,1)}), bf16[4,40,40,128]{3,2,1,0:T(8,128)(2,1)}, u32[]{:S(2)}, u32[]{:S(2)}) async-start(bf16[4,40,40,128]{3,2,1,0:T(8,128)(2,1)} %broadcast_in_dim.70), calls=%async_computation.7 | async-start | bytes 3276800 | tf_op jit(solution)/shard_map/all_to_all | solution.py:19
  274.2 3.2 copy-start
  455.4 27.6 %copy-start.1 = (f32[40,40,128]{2,1,0:T(8,128)S(1)}, f32[40,40,128]{2,1,0:T(8,128)}, u32[]{:S(2)}) copy-start(f32[40,40,128]{2,1,0:T(8,128)} %copy-done) | copy-start | bytes 2457604
  455.4 27.6 %copy-start.3 = (f32[40,40,128]{2,1,0:T(8,128)S(1)}, f32[40,40,128]{2,1,0:T(8,128)}, u32[]{:S(2)}) copy-start(f32[40,40,128]{2,1,0:T(8,128)} %get-tuple-element.34) | copy-start | bytes 2457604
where the time goes:
time: 493 us; the launch traced here: 485 us
  local copies, waits for them, and re-layouts  157 us (32%)
  blocking collectives  132 us (27%)
  other arithmetic  66.6 us (14%)
  waiting for transfers between devices  66.2 us (13%)
  starting transfers between devices  33.9 us (7%)
  matrix products  27.6 us (6%)
    unnamed x27, local copies, waits for them, and re-layouts  92.2 us
    all_to_all x1, blocking collectives, on_device(): lax.all_to_all(outgoing, ('row', 'col'), split_axis=2, concat_axis=2, til...  86.4 us
    all_to_all x1, waiting for transfers between devices, on_device(): lax.all_to_all(outgoing, ('row', 'col'), split_axis=2, concat_axis=2, til...  54.6 us
    all_to_all x1, blocking collectives, from_everyone(): return lax.all_to_all(copies, axis, split_axis=0, concat_axis=0, tiled=True)  25.6 us
    all_to_all x6, starting transfers between devices, from_everyone(): return lax.all_to_all(copies, axis, split_axis=0, concat_axis=0, tiled=True)  24.9 us
    unnamed x2, other arithmetic  22.9 us
    gather x2, local copies, waits for them, and re-layouts, on_device(): outgoing = jnp.take(sent_tiles, incoming, axis=2)  22.2 us
    dot_general x2, matrix products, on_device(): jnp.einsum('adcp,edcp->aecp', half_product, intersections, preferred_elem...  20.4 us
  transfers between devices with their start and end apart: 7, of which 3 were waited for; matrix products, arithmetic and copies ran while one was open for 29% of the time, Pallas kernels for 0%

commit v1 on v0

v1 whole, which is shorter than its diff:
```python
import functools
import math

import jax
import jax.numpy as jnp
from jax import lax
from jax.experimental import pallas as pl
from jax.experimental.pallas import tpu as pltpu
from jax.sharding import PartitionSpec as P

VMEM = pl.BlockSpec(memory_space=pltpu.VMEM)
SMEM = pl.BlockSpec(memory_space=pltpu.SMEM)
F32, BF16, I32 = jnp.float32, jnp.bfloat16, jnp.int32
NT = (((1,), (1,)), ((), ()))
TN = (((0,), (0,)), ((), ()))


def iota(shape, dim):
    return lax.broadcasted_iota(I32, shape, dim)


def request_kernel(cap, owner_ref, slot_ref, energy_ref, payload_ref, target_ref):
    links, pairs = owner_ref.shape
    groups = payload_ref.shape[0]
    before = (iota((pairs, pairs), 0) < iota((pairs, pairs), 1)).astype(BF16)
    base = jnp.zeros((groups, 1), F32)
    payload = jnp.zeros(payload_ref.shape, F32)
    for k in range(links):
        owner = owner_ref[k : k + 1, :]
        slot = slot_ref[k : k + 1, :].astype(F32)
        named = (iota((groups, pairs), 0) == owner).astype(F32)
        count = jnp.dot(named.astype(BF16), before, preferred_element_type=F32) + base
        place = jnp.sum(named * count, axis=0, keepdims=True).astype(I32)
        base = base + jnp.sum(named, axis=1, keepdims=True)
        target_ref[k : k + 1, :] = owner * cap + place
        placed = (iota((payload_ref.shape[1], pairs), 0) == place).astype(BF16)
        payload = payload + lax.dot_general(
            (named * slot).astype(BF16), placed, NT, preferred_element_type=F32
        )
    lane = iota(payload.shape, 1)
    for n in range(energy_ref.shape[0]):
        payload = jnp.where(lane == cap + n, energy_ref[n], payload)
    payload_ref[...] = payload


def gather_kernel(cap, payload_ref, sent_ref, out_ref, low, high):
    groups = payload_ref.shape[0]
    cells, pairs = sent_ref.shape
    slots = payload_ref[...].T.astype(I32)
    half = cap // 2
    for g in range(groups):
        column = slots[:cap, g : g + 1]
        hit = (iota((cap, pairs), 1) == column).astype(F32)
        low[g] = hit[:half]
        high[g] = hit[half:]
    low_hits, high_hits = low[...], high[...]
    hits = jnp.concatenate([low_hits, high_hits], axis=1).reshape(groups * cap, pairs).astype(BF16)
    whole = cells // 128
    for n in range(whole):
        block = lax.dot_general(
            hits, sent_ref[n * 128 : (n + 1) * 128, :], NT, preferred_element_type=F32
        )
        out_ref[:, n * cap : (n + 1) * cap, :] = block.astype(BF16).reshape(groups, cap, 128)
    rest = sent_ref[whole * 128 :, :]
    none = jnp.zeros((128 - rest.shape[0], pairs), BF16)
    low_hits = low_hits.reshape(groups * half, pairs).astype(BF16)
    high_hits = high_hits.reshape(groups * half, pairs).astype(BF16)
    block = lax.dot_general(
        low_hits, jnp.concatenate([rest, none], axis=0), NT, preferred_element_type=F32
    ) + lax.dot_general(
        high_hits, jnp.concatenate([none, rest], axis=0), NT, preferred_element_type=F32
    )
    out_ref[:, whole * cap :, :] = block.astype(BF16).reshape(groups, half, 128)


def select_kernel(cap, target_ref, back_ref, out_ref):
    groups = back_ref.shape[0]
    links, pairs = target_ref.shape
    half = cap // 2
    cells = out_ref.shape[1]
    whole = cells // 128
    rest = cells - whole * 128
    target = jnp.concatenate([target_ref[k : k + 1, :] for k in range(links)], axis=1)
    picks = (iota((groups * cap, links * pairs), 0) == target).astype(BF16)
    for n in range(whole):
        rows = back_ref[:, n * cap : (n + 1) * cap, :].reshape(groups * cap, 128)
        block = lax.dot_general(rows, picks, TN, preferred_element_type=F32).astype(BF16)
        for k in range(links):
            out_ref[k, n * 128 : (n + 1) * 128, :] = block[:, k * pairs : (k + 1) * pairs]
    rows = back_ref[:, whole * cap :, :].reshape(groups * half, 128)
    spot = iota((groups * half, links * pairs), 0)
    spot = (spot // half) * cap + spot % half
    low = lax.dot_general(rows, (spot == target).astype(BF16), TN, preferred_element_type=F32)
    high = lax.dot_general(
        rows, (spot + half == target).astype(BF16), TN, preferred_element_type=F32
    )
    block = (low[:rest] + high[rest:]).astype(BF16)
    for k in range(links):
        out_ref[k, whole * 128 :, :] = block[:, k * pairs : (k + 1) * pairs]


def call(kernel, out_shape, in_specs, scratch=(), flops=0, nbytes=0, many=False):
    return pl.pallas_call(
        kernel,
        out_shape=out_shape,
        in_specs=in_specs,
        out_specs=[VMEM] * len(out_shape) if many else VMEM,
        scratch_shapes=list(scratch),
        compiler_params=pltpu.CompilerParams(vmem_limit_bytes=48 * 2**20),
        cost_estimate=pl.CostEstimate(flops=flops, bytes_accessed=nbytes, transcendentals=0),
    )


def from_everyone(x, axis):
    copies = jnp.broadcast_to(x, (lax.axis_size(axis), *x.shape))
    return lax.all_to_all(copies, axis, split_axis=0, concat_axis=0, tiled=True)


def on_device(
    orbital_ints,
    occ_energy,
    pair_row,
    pair_col,
    virt_energy,
    amplitudes,
    intersections,
    coupling_fock,
    partner_owner,
    partner_slot,
):
    rows, cols = lax.axis_size("row"), lax.axis_size("col")
    groups = rows * cols
    size, _, pairs = amplitudes.shape
    cells = size * size
    links = partner_owner.shape[2]
    cap = 2 * pairs * links // groups
    chunk = cap * cells // 128
    per_block = orbital_ints.shape[0]

    payload, target = call(
        functools.partial(request_kernel, cap),
        [jax.ShapeDtypeStruct((groups, 128), F32), jax.ShapeDtypeStruct((links, pairs), I32)],
        [VMEM, VMEM, SMEM],
        flops=10**7,
        nbytes=10**5,
        many=True,
    )(partner_owner[0].T, partner_slot[0].T, occ_energy)
    incoming = lax.all_to_all(payload, ("row", "col"), split_axis=0, concat_axis=0, tiled=True)

    gather = call(
        functools.partial(gather_kernel, cap),
        jax.ShapeDtypeStruct((groups, chunk, 128), BF16),
        [VMEM, VMEM],
        scratch=[pltpu.VMEM((groups, cap // 2, pairs), F32)] * 2,
        flops=2 * groups * cap * cells * pairs,
        nbytes=2 * groups * cap * cells,
    )
    select = call(
        functools.partial(select_kernel, cap),
        jax.ShapeDtypeStruct((links, cells, pairs), BF16),
        [VMEM, VMEM],
        flops=2 * groups * cap * cells * pairs * links,
        nbytes=4 * groups * cap * cells,
    )

    def exchange(current):
        outgoing = gather(incoming, current.astype(BF16).reshape(cells, pairs))
        returned = lax.all_to_all(
            outgoing, ("row", "col"), split_axis=0, concat_axis=0, tiled=True
        )
        return select(target, returned).reshape(links, size, size, pairs)

    def coupling_of(tiles):
        half_product = jnp.einsum(
            "abcp,cbdp->adcp", intersections, tiles, preferred_element_type=F32
        ).astype(BF16)
        coupled = jnp.einsum(
            "adcp,edcp->aecp", half_product, intersections, preferred_element_type=F32
        )
        return jnp.sum(coupled * coupling_fock[None, None, :, :], axis=2)

    def sum_over_fit(x):
        return from_everyone(x.astype(BF16), "fit").astype(F32).sum(axis=0)

    tiles = exchange(amplitudes)

    row_ints = from_everyone(orbital_ints, "col").reshape(cols * per_block, *orbital_ints.shape[1:])
    col_ints = from_everyone(orbital_ints, "row").reshape(rows * per_block, *orbital_ints.shape[1:])
    kernel = jnp.einsum(
        "pax,pbx->abp",
        row_ints[pair_row],
        col_ints[pair_col],
        preferred_element_type=F32,
    )
    energies = incoming[:, cap : cap + per_block].reshape(rows, cols, per_block)
    row_energy = lax.dynamic_index_in_dim(energies, lax.axis_index("row"), 0, False).reshape(-1)
    col_energy = lax.dynamic_index_in_dim(energies, lax.axis_index("col"), 1, False).reshape(-1)

    def picked(table, index):
        hit = index[None, :] == jnp.arange(table.shape[0], dtype=I32)[:, None]
        return jnp.sum(jnp.where(hit, table[:, None], 0.0), axis=0)

    occupied = picked(row_energy, pair_row) + picked(col_energy, pair_col)
    denominator = virt_energy[:, None, :] + virt_energy[None, :, :] - occupied[None, None, :]

    first = coupling_of(tiles)
    current = sum_over_fit(first - kernel) / denominator
    second = coupling_of(exchange(current))
    residual = sum_over_fit(first - second)
    return (current - residual / denominator, residual)


def solution(mesh):
    placed = (
        P(("row", "col"), None, "fit"),
        P(("row", "col")),
        P(("row", "col")),
        P(("row", "col")),
        P(None, ("row", "col")),
        P(None, None, ("row", "col")),
        P(None, None, "fit", ("row", "col")),
        P("fit", ("row", "col")),
        P("fit", ("row", "col"), None),
        P("fit", ("row", "col"), None),
    )
    return jax.shard_map(
        on_device,
        mesh=mesh,
        in_specs=placed,
        out_specs=(P(None, None, ("row", "col")), P(None, None, ("row", "col"))),
        check_vma=False,
    )
```

time: 493 us -> 334 us (0.68); the launches traced: 485 us -> 333 us
  local copies, waits for them, and re-layouts: 157 us -> 42.9 us
  other arithmetic: 66.6 us -> 6.13 us
  waiting for transfers between devices: 66.2 us -> 87.1 us
  starting transfers between devices: 33.9 us -> 15 us
  blocking collectives: 132 us -> 144 us
  Pallas kernels: 0 us -> 9.43 us
    unnamed x27 -> x23, local copies, waits for them, and re-layouts: 92.2 us -> 10.7 us
    gather x8 -> x2, local copies, waits for them, and re-layouts: 47.6 us -> 10.5 us  [the longest x1 5.28 us: on_device(): col_ints[pair_col]]
    all_to_all x6 -> x2, waiting for transfers between devices: 11.6 us -> 39.1 us  [from_everyone(): return lax.all_to_all(copies, axis, split_axis=0, concat_axis=0, tiled=True)]
    unnamed x2 -> x0, other arithmetic: 22.9 us -> none
    add x1 -> x2, other arithmetic: 19.9 us -> 0.06 us  [the longest x1 0.06 us: on_device(): virt_energy[:, None, :] + virt_energy[None, :, :] - occupied[None, None, :]]
    all_to_all x1 -> x2, blocking collectives: 25.6 us -> 41.5 us  [from_everyone(): return lax.all_to_all(copies, axis, split_axis=0, concat_axis=0, tiled=True)]
    all_to_all x6 -> x2, starting transfers between devices: 24.9 us -> 9.34 us  [from_everyone(): return lax.all_to_all(copies, axis, split_axis=0, concat_axis=0, tiled=True)]
    select_n x5 -> x2, other arithmetic: 13.4 us -> 0.01 us  [the longest x1 0.01 us: on_device(): row_ints[pair_row]]
  transfers between devices with their start and end apart: 7 -> 3, of which waited for: 3 -> 3; matrix products, arithmetic and copies ran while one was open for 29% -> 9% of each run, Pallas kernels for 0% -> 1%
where the time goes in v1:
time: 334 us; the launch traced here: 333 us
  blocking collectives  144 us (43%)
  waiting for transfers between devices  87.1 us (26%)
  local copies, waits for them, and re-layouts  42.9 us (13%)
  matrix products  27.1 us (8%)
  starting transfers between devices  15 us (4%)
  Pallas kernels  9.43 us (3%)
  other arithmetic  6.13 us (2%)
    all_to_all x1, blocking collectives, exchange(): lax.all_to_all(outgoing, ('row', 'col'), split_axis=0, concat_axis=0, til...  83 us
    all_to_all x1, waiting for transfers between devices, exchange(): lax.all_to_all(outgoing, ('row', 'col'), split_axis=0, concat_axis=0, til...  48 us
    all_to_all x2, blocking collectives, from_everyone(): return lax.all_to_all(copies, axis, split_axis=0, concat_axis=0, tiled=True)  41.5 us
    all_to_all x2, waiting for transfers between devices, from_everyone(): return lax.all_to_all(copies, axis, split_axis=0, concat_axis=0, tiled=True)  39.1 us
    all_to_all x1, blocking collectives, on_device(): lax.all_to_all(payload, ('row', 'col'), split_axis=0, concat_axis=0, tile...  20 us
    dot_general x2, matrix products, coupling_of(): jnp.einsum('adcp,edcp->aecp', half_product, intersections, preferred_elem...  18.7 us
    reshape x2, local copies, waits for them, and re-layouts, exchange(): return select(target, returned).reshape(links, size, size, pairs)  11.5 us
    unnamed x23, local copies, waits for them, and re-layouts  10.7 us
  transfers between devices with their start and end apart: 3, of which 3 were waited for; matrix products, arithmetic and copies ran while one was open for 9% of the time, Pallas kernels for 1%

profile of v1, /device:TPU:32, one launch (start us, length us, event | category | flops | bytes accessed | tf_op | source)
XLA Modules:
  0.0 333.0 jit_solution(9149874375871258418)
XLA Ops:
  3.7 20.0 %all_to_all.41 = f32[64,1,128]{2,1,0:T(1,128)S(1)} all-to-all(f32[64,1,128]{2,1,0:T(1,128)S(1)} %bitcast.60), channel_id=1, replica_groups=mesh['row'=8,'col'=8,'fit'=4] {'row','col'}, dimensions={0} | all-to-all | bytes 65536 | tf_op jit(solution)/shard_map/all_to_all | solution.py:148
  23.8 1.8 broadcast_in_dim.47
  25.6 17.7 %all_to_all.42 = bf16[8,2,40,640]{3,2,1,0:T(8,128)(2,1)} all-to-all(bf16[8,2,40,640]{3,2,1,0:T(8,128)(2,1)} %broadcast_in_dim.47), channel_id=1, replica_groups=mesh['row'=8,'col'=8,'fit'=4] {'row'}, dimensions={0} | all-to-all | bytes 1638400 | tf_op jit(solution)/shard_map/all_to_all | solution.py:116
  43.3 4.9 %all-to-all-start.3 = ((bf16[8,2,40,640]{3,2,1,0:T(8,128)(2,1)}), bf16[8,2,40,640]{3,2,1,0:T(8,128)(2,1)S(1)}, u32[]{:S(2)}, u32[]{:S(2)}) async-start(bf16[8,2,40,640]{3,2,1,0:T(8,128)(2,1)} %broadcast_in_dim.47), calls=%async_computation.3 | async-start | bytes 1638400 | tf_op jit(solution)/shard_map/all_to_all | solution.py:116
  48.2 1.2 convert_element_type.31
  49.4 3.0 shard_map.114
  52.4 18.6 %all-to-all-done.3 = bf16[8,2,40,640]{3,2,1,0:T(8,128)(2,1)S(1)} async-done(((bf16[8,2,40,640]{3,2,1,0:T(8,128)(2,1)}), bf16[8,2,40,640]{3,2,1,0:T(8,128)(2,1)S(1)}, u32[]{:S(2)}, u32[]{:S(2)}) %all-to-all-start.3) | async-done | bytes 819232 | tf_op jit(solution)/shard_map/all_to_all | solution.py:116
  71.9 5.6 %all-to-all-start.1 = ((bf16[64,200,128]{2,1,0:T(8,128)(2,1)}), bf16[64,200,128]{2,1,0:T(8,128)(2,1)S(1)}, u32[]{:S(2)}, u32[]{:S(2)}) async-start(bf16[64,200,128]{2,1,0:T(8,128)(2,1)} %shard_map.114), calls=%async_computation.1 | async-start | bytes 6553600 | tf_op jit(solution)/shard_map/all_to_all | solution.py:168
  77.5 6.5 %copy.60 = bf16[40,40,4,128]{1,0,3,2:T(8,128)(2,1)} copy(bf16[40,40,4,128]{3,2,1,0:T(4,128)(2,1)} %param.16) | data formatting | bytes 3276800 | tf_op args[6]
  84.1 5.3 %gather_fusion = bf16[128,40,640]{2,1,0:T(8,128)(2,1)} fusion(bf16[16,40,640]{2,1,0:T(8,128)(2,1)} %bitcast.64, s32[1024]{0:T(1024)S(1)} %pad_clamp_fusion.1), kind=kCustom, calls=%fused_computation | custom fusion | bytes 13107712 | tf_op jit(solution)/shard_map/gather | solution.py:192
  89.3 5.2 %gather_fusion.1 = bf16[128,40,640]{2,1,0:T(8,128)(2,1)} fusion(bf16[16,40,640]{2,1,0:T(8,128)(2,1)} %bitcast.63, s32[1024]{0:T(1024)S(1)} %pad_clamp_fusion), kind=kCustom, calls=%fused_computation.1 | custom fusion | bytes 13107712 | tf_op jit(solution)/shard_map/gather | solution.py:191
  94.6 8.4 %fusion.18 = f32[128,40,40]{2,1,0:T(8,128)} fusion(bf16[128,40,640]{2,1,0:T(8,128)(2,1)} %gather_fusion, bf16[128,40,640]{2,1,0:T(8,128)(2,1)} %gather_fusion.1), kind=kOutput, calls=%fused_computation.34 | convolution fusion | flops 262144000 | bytes 13926400 | tf_op jit(solution)/shard_map/pax,pbx->abp/dot_general | solution.py:189
  103.0 3.1 copy.64
  106.1 48.0 %all-to-all-done.1.back_ref = bf16[64,200,128]{2,1,0:T(8,128)(2,1)S(1)} async-done(((bf16[64,200,128]{2,1,0:T(8,128)(2,1)}), bf16[64,200,128]{2,1,0:T(8,128)(2,1)S(1)}, u32[]{:S(2)}, u32[]{:S(2)}) %all-to-all-start.1) | async-done | bytes 3276832 | tf_op jit(solution)/shard_map/all_to_all | solution.py:168
  154.1 2.0 shard_map.115
  156.1 1.2 copy-done
  157.4 6.5 %copy.59 = bf16[4,40,40,128]{1,2,3,0:T(8,128)(2,1)} copy(bf16[4,40,40,128]{3,2,1,0:T(8,128)(2,1)} %bitcast.56) | data formatting | bytes 3276800 | tf_op jit(solution)/shard_map/reshape | solution.py:171
  163.9 9.4 %multiply_reduce_fusion.1 = f32[128,40,40]{2,1,0:T(8,128)S(1)} fusion(f32[4,128]{1,0:T(4,128)S(1)} %copy-done.8, bf16[40,40,4,128]{1,0,3,2:T(8,128)(2,1)} %copy.60, bf16[4,40,40,128]{1,2,3,0:T(8,128)(2,1)} %copy.59), kind=kOutput, calls=%fused_computation.3 | convolution fusion | flops 133324800 | bytes 4098048 | tf_op jit(solution)/shard_map/adcp,edcp->aecp/dot_general | solution.py:177
  173.3 1.6 copy.63
  174.9 1.5 fusion.17
  176.4 1.4 broadcast_in_dim.50
  177.8 4.5 %all-to-all-start.4 = ((bf16[4,40,40,128]{3,2,1,0:T(8,128)(2,1)}), bf16[4,40,40,128]{3,2,1,0:T(8,128)(2,1)S(1)}, u32[]{:S(2)}, u32[]{:S(2)}) async-start(bf16[4,40,40,128]{3,2,1,0:T(8,128)(2,1)} %broadcast_in_dim.50), calls=%async_computation.4 | async-start | bytes 3276800 | tf_op jit(solution)/shard_map/all_to_all | solution.py:116
  182.7 20.6 %all-to-all-done.4 = bf16[4,40,40,128]{3,2,1,0:T(8,128)(2,1)S(1)} async-done(((bf16[4,40,40,128]{3,2,1,0:T(8,128)(2,1)}), bf16[4,40,40,128]{3,2,1,0:T(8,128)(2,1)S(1)}, u32[]{:S(2)}, u32[]{:S(2)}) %all-to-all-start.4) | async-done | bytes 1638432 | tf_op jit(solution)/shard_map/all_to_all | solution.py:116
  203.7 1.3 shard_map.116
  205.0 83.0 %all_to_all.43.back_ref = bf16[64,200,128]{2,1,0:T(8,128)(2,1)S(1)} all-to-all(bf16[64,200,128]{2,1,0:T(8,128)(2,1)S(1)} %shard_map.116), channel_id=1, replica_groups=mesh['row'=8,'col'=8,'fit'=4] {'row','col'}, dimensions={0} | all-to-all | bytes 6553600 | tf_op jit(solution)/shard_map/all_to_all | solution.py:168
  288.0 2.0 shard_map.117
  290.0 5.0 %copy.68 = bf16[4,40,40,128]{1,2,3,0:T(8,128)(2,1)} copy(bf16[4,40,40,128]{3,2,1,0:T(8,128)(2,1)S(1)} %bitcast.55) | data formatting | bytes 3276800 | tf_op jit(solution)/shard_map/reshape | solution.py:171
  295.0 9.3 %multiply_reduce_fusion = f32[128,40,40]{2,1,0:T(8,128)S(1)} fusion(f32[4,128]{1,0:T(4,128)S(1)} %copy-done.8, bf16[40,40,4,128]{1,0,3,2:T(8,128)(2,1)} %copy.60, bf16[4,40,40,128]{1,2,3,0:T(8,128)(2,1)} %copy.68), kind=kOutput, calls=%fused_computation.2 | convolution fusion | flops 133324800 | bytes 4098048 | tf_op jit(solution)/shard_map/adcp,edcp->aecp/dot_general | solution.py:177
  304.3 1.8 copy.72
  306.1 1.5 fusion.14
  307.8 23.8 %all_to_all.44 = bf16[4,40,40,128]{3,2,1,0:T(8,128)(2,1)S(1)} all-to-all(bf16[4,40,40,128]{3,2,1,0:T(8,128)(2,1)S(1)} %broadcast_in_dim.56), channel_id=1, replica_groups=mesh['row'=8,'col'=8,'fit'=4] {'fit'}, dimensions={0} | all-to-all | bytes 3276800 | tf_op jit(solution)/shard_map/all_to_all | solution.py:116
  331.9 1.2 divide_subtract_fusion
  (38 shorter events, 5.2 us)
Async XLA Ops:
  0.6 0.7 copy-start.1
  1.3 0.7 copy-start.2
  2.0 0.7 copy-start.3
  43.3 27.6 %all-to-all-start.3 = ((bf16[8,2,40,640]{3,2,1,0:T(8,128)(2,1)}), bf16[8,2,40,640]{3,2,1,0:T(8,128)(2,1)S(1)}, u32[]{:S(2)}, u32[]{:S(2)}) async-start(bf16[8,2,40,640]{3,2,1,0:T(8,128)(2,1)} %broadcast_in_dim.47), calls=%async_computation.3 | async-start | bytes 1638400 | tf_op jit(solution)/shard_map/all_to_all | solution.py:116
  52.4 31.6 %copy-start.9 = (s32[128]{0:T(128)S(1)}, s32[128]{0:T(128)}, u32[]{:S(2)}) copy-start(s32[128]{0:T(128)} %param.13) | copy-start | bytes 1540
  52.4 31.6 %copy-start.10 = (s32[128]{0:T(128)S(1)}, s32[128]{0:T(128)}, u32[]{:S(2)}) copy-start(s32[128]{0:T(128)} %param.12) | copy-start | bytes 1540
  71.0 0.9 copy-start.4
  71.9 82.2 %all-to-all-start.1 = ((bf16[64,200,128]{2,1,0:T(8,128)(2,1)}), bf16[64,200,128]{2,1,0:T(8,128)(2,1)S(1)}, u32[]{:S(2)}, u32[]{:S(2)}) async-start(bf16[64,200,128]{2,1,0:T(8,128)(2,1)} %shard_map.114), calls=%async_computation.1 | async-start | bytes 6553600 | tf_op jit(solution)/shard_map/all_to_all | solution.py:168
  154.1 9.8 %copy-start.8 = (f32[4,128]{1,0:T(4,128)S(1)}, f32[4,128]{1,0:T(4,128)}, u32[]{:S(2)}) copy-start(f32[4,128]{1,0:T(4,128)} %param.17) | copy-start | bytes 6148
  156.1 1.2 copy-start
  173.3 9.0 %copy-start.7 = (f32[40,128]{1,0:T(8,128)S(1)}, f32[40,128]{1,0:T(8,128)}, u32[]{:S(2)}) copy-start(f32[40,128]{1,0:T(8,128)} %param.14) | copy-start | bytes 61444
  174.9 7.8 %copy-start.5 = (f32[128,40,40]{0,2,1:T(8,128)}, f32[128,40,40]{0,2,1:T(8,128)S(1)}, u32[]{:S(2)}) copy-start(f32[128,40,40]{0,2,1:T(8,128)S(1)} %copy.63) | copy-start | bytes 2457604
  177.8 25.5 %all-to-all-start.4 = ((bf16[4,40,40,128]{3,2,1,0:T(8,128)(2,1)}), bf16[4,40,40,128]{3,2,1,0:T(8,128)(2,1)S(1)}, u32[]{:S(2)}, u32[]{:S(2)}) async-start(bf16[4,40,40,128]{3,2,1,0:T(8,128)(2,1)} %broadcast_in_dim.50), calls=%async_computation.4 | async-start | bytes 3276800 | tf_op jit(solution)/shard_map/all_to_all | solution.py:116
  331.8 1.2 copy-start.6

commit v2 on v1

--- a/solution.py
+++ b/solution.py
@@ -1,5 +1,4 @@
 import functools
-import math
 
 import jax
 import jax.numpy as jnp
@@ -116,6 +115,28 @@
     return lax.all_to_all(copies, axis, split_axis=0, concat_axis=0, tiled=True)
 
 
+def shifted(x, axis, step):
+    count = lax.axis_size(axis)
+    return lax.ppermute(x, axis, [(n, (n + step) % count) for n in range(count)])
+
+
+def ring_copies(x, axis, step=1):
+    length = lax.axis_size(axis) // step
+    ahead, behind = [x], [x]
+    for n in range(length // 2):
+        ahead.append(shifted(ahead[-1], axis, step))
+        if n < length - 1 - length // 2:
+            behind.append(shifted(behind[-1], axis, -step))
+    return jnp.stack(ahead + behind[:0:-1])
+
+
+def chip_ring_copies(x, axis):
+    count = lax.axis_size(axis)
+    mine = ring_copies(x, axis, 2)
+    theirs = lax.ppermute(mine, axis, [(n, n ^ 1) for n in range(count)])
+    return jnp.concatenate([mine, theirs])
+
+
 def on_device(
     orbital_ints,
     occ_energy,
@@ -163,12 +184,14 @@
         nbytes=4 * groups * cap * cells,
     )
 
-    def exchange(current):
-        outgoing = gather(incoming, current.astype(BF16).reshape(cells, pairs))
+    def returned_tiles(outgoing):
         returned = lax.all_to_all(
             outgoing, ("row", "col"), split_axis=0, concat_axis=0, tiled=True
         )
         return select(target, returned).reshape(links, size, size, pairs)
+
+    def outgoing_tiles(current):
+        return gather(incoming, current.astype(BF16).reshape(cells, pairs))
 
     def coupling_of(tiles):
         half_product = jnp.einsum(
@@ -182,19 +205,26 @@
     def sum_over_fit(x):
         return from_everyone(x.astype(BF16), "fit").astype(F32).sum(axis=0)
 
-    tiles = exchange(amplitudes)
-
-    row_ints = from_everyone(orbital_ints, "col").reshape(cols * per_block, *orbital_ints.shape[1:])
-    col_ints = from_everyone(orbital_ints, "row").reshape(rows * per_block, *orbital_ints.shape[1:])
+    outgoing, own_ints = lax.optimization_barrier((outgoing_tiles(amplitudes), orbital_ints))
+    tiles = returned_tiles(outgoing)
+
+    row_ints = ring_copies(own_ints, "col").reshape(-1, *orbital_ints.shape[1:])
+    col_ints = chip_ring_copies(own_ints, "row").reshape(-1, *orbital_ints.shape[1:])
+    owner_col, inner_row = pair_row // per_block, pair_row % per_block
+    owner_row, inner_col = pair_col // per_block, pair_col % per_block
+    my_row, my_col = lax.axis_index("row"), lax.axis_index("col")
+    back = (my_col - owner_col) % cols
+    chips_back = (my_row // 2 - owner_row // 2) % (rows // 2)
+    other_core = (my_row + owner_row) % 2
     kernel = jnp.einsum(
         "pax,pbx->abp",
-        row_ints[pair_row],
-        col_ints[pair_col],
+        row_ints[back * per_block + inner_row],
+        col_ints[(other_core * (rows // 2) + chips_back) * per_block + inner_col],
         preferred_element_type=F32,
     )
     energies = incoming[:, cap : cap + per_block].reshape(rows, cols, per_block)
-    row_energy = lax.dynamic_index_in_dim(energies, lax.axis_index("row"), 0, False).reshape(-1)
-    col_energy = lax.dynamic_index_in_dim(energies, lax.axis_index("col"), 1, False).reshape(-1)
+    row_energy = lax.dynamic_index_in_dim(energies, my_row, 0, False).reshape(-1)
+    col_energy = lax.dynamic_index_in_dim(energies, my_col, 1, False).reshape(-1)
 
     def picked(table, index):
         hit = index[None, :] == jnp.arange(table.shape[0], dtype=I32)[:, None]
@@ -205,7 +235,7 @@
 
     first = coupling_of(tiles)
     current = sum_over_fit(first - kernel) / denominator
-    second = coupling_of(exchange(current))
+    second = coupling_of(returned_tiles(outgoing_tiles(current)))
     residual = sum_over_fit(first - second)
     return (current - residual / denominator, residual)
 

time: 334 us -> 336 us (level)
  blocking collectives: 144 us -> 111 us
  starting transfers between devices: 15 us -> 36.2 us
  local copies, waits for them, and re-layouts: 42.9 us -> 51.3 us
  waiting for transfers between devices: 87.1 us -> 91.5 us
    ppermute x0 -> x11, waiting for transfers between devices: none -> 64.6 us  [the longest x10 64.6 us: shifted(): lax.ppermute(x, axis, [(n, (n + step) % count) for n in range(count)])]
    all_to_all x1 -> x2, waiting for transfers between devices: 48 us -> 7.37 us  [the longest x1 7.37 us: on_device(): lax.all_to_all(payload, ('row', 'col'), split_axis=0, concat_axis=0, tile...]
    all_to_all x2 -> x1, waiting for transfers between devices: 39.1 us -> 19.5 us  [from_everyone(): return lax.all_to_all(copies, axis, split_axis=0, concat_axis=0, tiled=True)]
    all_to_all x2 -> x1, blocking collectives: 41.5 us -> 23.8 us  [from_everyone(): return lax.all_to_all(copies, axis, split_axis=0, concat_axis=0, tiled=True)]
    all_to_all x2 -> x1, blocking collectives: 103 us -> 86.9 us  [returned_tiles(): lax.all_to_all(outgoing, ('row', 'col'), split_axis=0, concat_axis=0, til...]
    ppermute x0 -> x11, starting transfers between devices: none -> 14.4 us  [the longest x10 14.4 us: shifted(): lax.ppermute(x, axis, [(n, (n + step) % count) for n in range(count)])]
    all_to_all x1 -> x2, starting transfers between devices: 5.63 us -> 17.3 us  [the longest x1 11.6 us: on_device(): lax.all_to_all(payload, ('row', 'col'), split_axis=0, concat_axis=0, tile...]
    unnamed x23 -> x34, local copies, waits for them, and re-layouts: 10.7 us -> 18.4 us
  transfers between devices with their start and end apart: 3 -> 14, of which waited for: 3 -> 6; matrix products, arithmetic and copies ran while one was open for 9% -> 13% of each run, Pallas kernels for 1% -> 0%
where the time goes in v2:
time: 336 us; the launch traced here: 335 us
  blocking collectives  111 us (33%)
  waiting for transfers between devices  91.5 us (27%)
  local copies, waits for them, and re-layouts  51.3 us (15%)
  starting transfers between devices  36.2 us (11%)
  matrix products  27.2 us (8%)
  Pallas kernels  10.1 us (3%)
  other arithmetic  7.01 us (2%)
    all_to_all x1, blocking collectives, returned_tiles(): lax.all_to_all(outgoing, ('row', 'col'), split_axis=0, concat_axis=0, til...  86.9 us
    ppermute x10, waiting for transfers between devices, shifted(): lax.ppermute(x, axis, [(n, (n + step) % count) for n in range(count)])  64.6 us
    all_to_all x1, blocking collectives, from_everyone(): return lax.all_to_all(copies, axis, split_axis=0, concat_axis=0, tiled=True)  23.8 us
    all_to_all x1, waiting for transfers between devices, from_everyone(): return lax.all_to_all(copies, axis, split_axis=0, concat_axis=0, tiled=True)  19.5 us
    dot_general x2, matrix products, coupling_of(): jnp.einsum('adcp,edcp->aecp', half_product, intersections, preferred_elem...  18.8 us
    unnamed x34, local copies, waits for them, and re-layouts  18.4 us
    ppermute x10, starting transfers between devices, shifted(): lax.ppermute(x, axis, [(n, (n + step) % count) for n in range(count)])  14.4 us
    all_to_all x1, starting transfers between devices, on_device(): lax.all_to_all(payload, ('row', 'col'), split_axis=0, concat_axis=0, tile...  11.6 us
  transfers between devices with their start and end apart: 14, of which 6 were waited for; matrix products, arithmetic and copies ran while one was open for 13% of the time, Pallas kernels for 0%

profile of v2, /device:TPU:32, one launch (start us, length us, event | category | flops | bytes accessed | tf_op | source)
XLA Modules:
  0.0 334.8 jit_solution(4214877659991605370)
XLA Ops:
  2.7 1.7 shard_map.113
  4.3 11.6 %all-to-all-start = ((f32[64,1,128]{2,1,0:T(1,128)}), f32[64,1,128]{2,1,0:T(1,128)S(1)}, u32[]{:S(2)}, u32[]{:S(2)}) async-start(f32[64,1,128]{2,1,0:T(1,128)} %bitcast.5), calls=%async_computation | async-start | bytes 65536 | tf_op jit(solution)/shard_map/all_to_all | solution.py:169
  17.2 7.4 %all-to-all-done = f32[64,1,128]{2,1,0:T(1,128)S(1)} async-done(((f32[64,1,128]{2,1,0:T(1,128)}), f32[64,1,128]{2,1,0:T(1,128)S(1)}, u32[]{:S(2)}, u32[]{:S(2)}) %all-to-all-start) | async-done | bytes 32800 | tf_op jit(solution)/shard_map/all_to_all | solution.py:169
  24.5 3.0 shard_map.114
  27.5 5.7 %all-to-all-start.1 = ((bf16[64,200,128]{2,1,0:T(8,128)(2,1)}), bf16[64,200,128]{2,1,0:T(8,128)(2,1)S(1)}, u32[]{:S(2)}, u32[]{:S(2)}) async-start(bf16[64,200,128]{2,1,0:T(8,128)(2,1)} %shard_map.114), calls=%async_computation.1 | async-start | bytes 6553600 | tf_op jit(solution)/shard_map/all_to_all | solution.py:188
  33.3 6.5 %copy.60 = bf16[40,40,4,128]{1,0,3,2:T(8,128)(2,1)} copy(bf16[40,40,4,128]{3,2,1,0:T(4,128)(2,1)} %param.16) | data formatting | bytes 3276800 | tf_op args[6]
  41.4 1.6 collective-permute-start
  44.2 1.7 collective-permute-start.2
  45.9 2.1 copy.83
  48.0 59.0 %collective-permute-done.4 = bf16[2,40,640]{2,1,0:T(8,128)(2,1)S(1)} collective-permute-done((bf16[2,40,640]{2,1,0:T(8,128)(2,1)S(1)}, bf16[2,40,640]{2,1,0:T(8,128)(2,1)S(1)}, u32[]{:S(2)}, u32[]{:S(2)}) %collective-permute-start.4) | collective-permute-done | bytes 102432 | tf_op jit(solution)/shard_map/ppermute | solution.py:120
  108.4 1.7 collective-permute-start.1
  112.7 1.7 collective-permute-done.1
  120.5 1.7 collective-permute-start.7
  122.8 3.6 %collective-permute-done.7 = bf16[2,40,640]{2,1,0:T(8,128)(2,1)S(1)} collective-permute-done((bf16[2,40,640]{2,1,0:T(8,128)(2,1)S(1)}, bf16[2,40,640]{2,1,0:T(8,128)(2,1)S(1)}, u32[]{:S(2)}, u32[]{:S(2)}) %collective-permute-start.7) | collective-permute-done | bytes 102432 | tf_op jit(solution)/shard_map/ppermute | solution.py:120
  129.0 5.3 %gather_fusion.1 = bf16[128,40,640]{2,1,0:T(8,128)(2,1)} fusion(bf16[16,40,640]{2,1,0:T(8,128)(2,1)} %bitcast.23, s32[1024]{0:T(1024)S(1)} %get-tuple-element.10), kind=kCustom, calls=%fused_computation.1 | custom fusion | bytes 13107712 | tf_op jit(solution)/shard_map/gather | solution.py:221
  134.3 1.8 constant_dynamic-update-slice_fusion
  136.1 5.3 %gather_fusion = bf16[128,40,640]{2,1,0:T(8,128)(2,1)} fusion(bf16[16,40,640]{2,1,0:T(8,128)(2,1)} %bitcast.15, s32[1024]{0:T(1024)S(1)} %get-tuple-element.11), kind=kCustom, calls=%fused_computation | custom fusion | bytes 13107712 | tf_op jit(solution)/shard_map/gather | solution.py:222
  141.4 8.5 %fusion.26 = f32[128,40,40]{2,1,0:T(8,128)} fusion(bf16[128,40,640]{2,1,0:T(8,128)(2,1)} %gather_fusion, bf16[128,40,640]{2,1,0:T(8,128)(2,1)} %gather_fusion.1), kind=kOutput, calls=%fused_computation.79 | convolution fusion | flops 262144000 | bytes 13926400 | tf_op jit(solution)/shard_map/pax,pbx->abp/dot_general | solution.py:219
  149.8 3.1 copy.64
  152.9 2.1 shard_map.115
  156.2 6.6 %copy.59 = bf16[4,40,40,128]{1,2,3,0:T(8,128)(2,1)} copy(bf16[4,40,40,128]{3,2,1,0:T(8,128)(2,1)} %bitcast.79) | data formatting | bytes 3276800 | tf_op jit(solution)/shard_map/reshape | solution.py:191
  162.8 9.4 %multiply_reduce_fusion.1 = f32[128,40,40]{2,1,0:T(8,128)S(1)} fusion(f32[4,128]{1,0:T(4,128)S(1)} %copy-done.8, bf16[40,40,4,128]{1,0,3,2:T(8,128)(2,1)} %copy.60, bf16[4,40,40,128]{1,2,3,0:T(8,128)(2,1)} %copy.59), kind=kOutput, calls=%fused_computation.3 | convolution fusion | flops 133324800 | bytes 4098048 | tf_op jit(solution)/shard_map/adcp,edcp->aecp/dot_general | solution.py:200
  172.2 1.6 copy.63
  173.8 1.6 fusion.17
  176.7 4.5 %all-to-all-start.2 = ((bf16[4,40,40,128]{3,2,1,0:T(8,128)(2,1)}), bf16[4,40,40,128]{3,2,1,0:T(8,128)(2,1)S(1)}, u32[]{:S(2)}, u32[]{:S(2)}) async-start(bf16[4,40,40,128]{3,2,1,0:T(8,128)(2,1)} %broadcast_in_dim.45), calls=%async_computation.2 | async-start | bytes 3276800 | tf_op jit(solution)/shard_map/all_to_all | solution.py:115
  181.6 19.5 %all-to-all-done.2 = bf16[4,40,40,128]{3,2,1,0:T(8,128)(2,1)S(1)} async-done(((bf16[4,40,40,128]{3,2,1,0:T(8,128)(2,1)}), bf16[4,40,40,128]{3,2,1,0:T(8,128)(2,1)S(1)}, u32[]{:S(2)}, u32[]{:S(2)}) %all-to-all-start.2) | async-done | bytes 1638432 | tf_op jit(solution)/shard_map/all_to_all | solution.py:115
  202.8 86.9 %all_to_all.31.back_ref = bf16[64,200,128]{2,1,0:T(8,128)(2,1)S(1)} all-to-all(bf16[64,200,128]{2,1,0:T(8,128)(2,1)S(1)} %shard_map.116), channel_id=1, replica_groups=mesh['row'=8,'col'=8,'fit'=4] {'row','col'}, dimensions={0} | all-to-all | bytes 6553600 | tf_op jit(solution)/shard_map/all_to_all | solution.py:188
  289.7 2.1 shard_map.117
  291.7 5.0 %copy.68 = bf16[4,40,40,128]{1,2,3,0:T(8,128)(2,1)} copy(bf16[4,40,40,128]{3,2,1,0:T(8,128)(2,1)S(1)} %bitcast.78) | data formatting | bytes 3276800 | tf_op jit(solution)/shard_map/reshape | solution.py:191
  296.7 9.4 %multiply_reduce_fusion = f32[128,40,40]{2,1,0:T(8,128)S(1)} fusion(f32[4,128]{1,0:T(4,128)S(1)} %copy-done.8, bf16[40,40,4,128]{1,0,3,2:T(8,128)(2,1)} %copy.60, bf16[4,40,40,128]{1,2,3,0:T(8,128)(2,1)} %copy.68), kind=kOutput, calls=%fused_computation.2 | convolution fusion | flops 133324800 | bytes 4098048 | tf_op jit(solution)/shard_map/adcp,edcp->aecp/dot_general | solution.py:200
  306.1 1.8 copy.72
  309.6 23.8 %all_to_all.32 = bf16[4,40,40,128]{3,2,1,0:T(8,128)(2,1)S(1)} all-to-all(bf16[4,40,40,128]{3,2,1,0:T(8,128)(2,1)S(1)} %broadcast_in_dim.51), channel_id=1, replica_groups=mesh['row'=8,'col'=8,'fit'=4] {'fit'}, dimensions={0} | all-to-all | bytes 3276800 | tf_op jit(solution)/shard_map/all_to_all | solution.py:115
  (70 shorter events, 27.2 us)
Async XLA Ops:
  0.6 0.7 copy-start.1
  1.3 0.7 copy-start.2
  2.0 0.7 copy-start.3
  4.3 20.2 %all-to-all-start = ((f32[64,1,128]{2,1,0:T(1,128)}), f32[64,1,128]{2,1,0:T(1,128)S(1)}, u32[]{:S(2)}, u32[]{:S(2)}) async-start(f32[64,1,128]{2,1,0:T(1,128)} %bitcast.5), calls=%async_computation | async-start | bytes 65536 | tf_op jit(solution)/shard_map/all_to_all | solution.py:169
  27.5 12.3 %copy-start.9 = (s32[128]{0:T(128)S(1)}, s32[128]{0:T(128)}, u32[]{:S(2)}) copy-start(s32[128]{0:T(128)} %param.13) | copy-start | bytes 1540
  27.5 12.3 %copy-start.10 = (s32[128]{0:T(128)S(1)}, s32[128]{0:T(128)}, u32[]{:S(2)}) copy-start(s32[128]{0:T(128)} %param.12) | copy-start | bytes 1540
  27.5 12.3 %copy-start.6 = (bf16[2,40,640]{2,1,0:T(8,128)(2,1)S(1)}, bf16[2,40,640]{2,1,0:T(8,128)(2,1)}, u32[]{:S(2)}) copy-start(bf16[2,40,640]{2,1,0:T(8,128)(2,1)} %param.10) | copy-start | bytes 307204
  27.5 125.4 %all-to-all-start.1 = ((bf16[64,200,128]{2,1,0:T(8,128)(2,1)}), bf16[64,200,128]{2,1,0:T(8,128)(2,1)S(1)}, u32[]{:S(2)}, u32[]{:S(2)}) async-start(bf16[64,200,128]{2,1,0:T(8,128)(2,1)} %shard_map.114), calls=%async_computation.1 | async-start | bytes 6553600 | tf_op jit(solution)/shard_map/all_to_all | solution.py:188
  39.9 67.1 %collective-permute-start.4 = (bf16[2,40,640]{2,1,0:T(8,128)(2,1)S(1)}, bf16[2,40,640]{2,1,0:T(8,128)(2,1)S(1)}, u32[]{:S(2)}, u32[]{:S(2)}) collective-permute-start(bf16[2,40,640]{2,1,0:T(8,128)(2,1)S(1)} %copy-done.6), channel_id=1, source_target_pairs={{0,4},{4,8},{8,12},{12,16},{16,20},{20,24},{24,28},{28,0},{1,5},{5... | collective-permute-start | bytes 307208 | tf_op jit(solution)/shard_map/ppermute | solution.py:120
  41.4 67.0 %collective-permute-start = (bf16[2,40,640]{2,1,0:T(8,128)(2,1)S(1)}, bf16[2,40,640]{2,1,0:T(8,128)(2,1)S(1)}, u32[]{:S(2)}, u32[]{:S(2)}) collective-permute-start(bf16[2,40,640]{2,1,0:T(8,128)(2,1)S(1)} %copy-done.6), channel_id=1, source_target_pairs={{0,64},{32,96},{64,128},{96,160},{128,192},{160,224},{192,0},{224,... | collective-permute-start | bytes 307208 | tf_op jit(solution)/shard_map/ppermute | solution.py:120
  43.6 67.8 %collective-permute-start.8 = (bf16[2,40,640]{2,1,0:T(8,128)(2,1)S(1)}, bf16[2,40,640]{2,1,0:T(8,128)(2,1)S(1)}, u32[]{:S(2)}, u32[]{:S(2)}) collective-permute-start(bf16[2,40,640]{2,1,0:T(8,128)(2,1)S(1)} %copy-done.6), channel_id=1, source_target_pairs={{0,28},{4,0},{8,4},{12,8},{16,12},{20,16},{24,20},{28,24},{1,29},{... | collective-permute-start | bytes 307208 | tf_op jit(solution)/shard_map/ppermute | solution.py:120
  44.2 68.5 %collective-permute-start.2 = (bf16[2,40,640]{2,1,0:T(8,128)(2,1)S(1)}, bf16[2,40,640]{2,1,0:T(8,128)(2,1)S(1)}, u32[]{:S(2)}, u32[]{:S(2)}) collective-permute-start(bf16[2,40,640]{2,1,0:T(8,128)(2,1)S(1)} %copy-done.6), channel_id=1, source_target_pairs={{0,192},{32,224},{64,0},{96,32},{128,64},{160,96},{192,128},{224,1... | collective-permute-start | bytes 307208 | tf_op jit(solution)/shard_map/ppermute | solution.py:120
  106.9 8.3 %collective-permute-start.5 = (bf16[2,40,640]{2,1,0:T(8,128)(2,1)S(1)}, bf16[2,40,640]{2,1,0:T(8,128)(2,1)S(1)}, u32[]{:S(2)}, u32[]{:S(2)}) collective-permute-start(bf16[2,40,640]{2,1,0:T(8,128)(2,1)S(1)} %collective-permute-done.4), channel_id=1, source_target_pairs={{0,4},{4,8},{8,12},{12,16},{16,20},{20,24},{24,28},{28,0},{1,5},{5... | collective-permute-start | bytes 307208 | tf_op jit(solution)/shard_map/ppermute | solution.py:120
  108.4 6.0 %collective-permute-start.1 = (bf16[2,40,640]{2,1,0:T(8,128)(2,1)S(1)}, bf16[2,40,640]{2,1,0:T(8,128)(2,1)S(1)}, u32[]{:S(2)}, u32[]{:S(2)}) collective-permute-start(bf16[2,40,640]{2,1,0:T(8,128)(2,1)S(1)} %collective-permute-done), channel_id=1, source_target_pairs={{0,64},{32,96},{64,128},{96,160},{128,192},{160,224},{192,0},{224,... | collective-permute-start | bytes 307208 | tf_op jit(solution)/shard_map/ppermute | solution.py:120
  111.4 5.3 %collective-permute-start.9 = (bf16[2,40,640]{2,1,0:T(8,128)(2,1)S(1)}, bf16[2,40,640]{2,1,0:T(8,128)(2,1)S(1)}, u32[]{:S(2)}, u32[]{:S(2)}) collective-permute-start(bf16[2,40,640]{2,1,0:T(8,128)(2,1)S(1)} %collective-permute-done.8), channel_id=1, source_target_pairs={{0,28},{4,0},{8,4},{12,8},{16,12},{20,16},{24,20},{28,24},{1,29},{... | collective-permute-start | bytes 307208 | tf_op jit(solution)/shard_map/ppermute | solution.py:120
  115.2 19.1 %collective-permute-start.3 = (bf16[4,2,40,640]{3,2,1,0:T(8,128)(2,1)}, bf16[4,2,40,640]{3,2,1,0:T(8,128)(2,1)}, u32[]{:S(2)}, u32[]{:S(2)}) collective-permute-start(bf16[4,2,40,640]{3,2,1,0:T(8,128)(2,1)} %pad_maximum_fusion), channel_id=1, source_target_pairs={{0,32},{32,0},{64,96},{96,64},{128,160},{160,128},{192,224},{224,1... | collective-permute-start | bytes 1228808 | tf_op jit(solution)/shard_map/ppermute | solution.py:136
  115.2 5.3 %collective-permute-start.6 = (bf16[2,40,640]{2,1,0:T(8,128)(2,1)S(1)}, bf16[2,40,640]{2,1,0:T(8,128)(2,1)S(1)}, u32[]{:S(2)}, u32[]{:S(2)}) collective-permute-start(bf16[2,40,640]{2,1,0:T(8,128)(2,1)S(1)} %collective-permute-done.5), channel_id=1, source_target_pairs={{0,4},{4,8},{8,12},{12,16},{16,20},{20,24},{24,28},{28,0},{1,5},{5... | collective-permute-start | bytes 307208 | tf_op jit(solution)/shard_map/ppermute | solution.py:120
  116.7 10.4 %collective-permute-start.10 = (bf16[2,40,640]{2,1,0:T(8,128)(2,1)S(1)}, bf16[2,40,640]{2,1,0:T(8,128)(2,1)S(1)}, u32[]{:S(2)}, u32[]{:S(2)}) collective-permute-start(bf16[2,40,640]{2,1,0:T(8,128)(2,1)S(1)} %collective-permute-done.9), channel_id=1, source_target_pairs={{0,28},{4,0},{8,4},{12,8},{16,12},{20,16},{24,20},{28,24},{1,29},{... | collective-permute-start | bytes 307208 | tf_op jit(solution)/shard_map/ppermute | solution.py:120
  120.5 5.9 %collective-permute-start.7 = (bf16[2,40,640]{2,1,0:T(8,128)(2,1)S(1)}, bf16[2,40,640]{2,1,0:T(8,128)(2,1)S(1)}, u32[]{:S(2)}, u32[]{:S(2)}) collective-permute-start(bf16[2,40,640]{2,1,0:T(8,128)(2,1)S(1)} %collective-permute-done.6), channel_id=1, source_target_pairs={{0,4},{4,8},{8,12},{12,16},{16,20},{20,24},{24,28},{28,0},{1,5},{5... | collective-permute-start | bytes 307208 | tf_op jit(solution)/shard_map/ppermute | solution.py:120
  152.9 9.9 %copy-start.8 = (f32[4,128]{1,0:T(4,128)S(1)}, f32[4,128]{1,0:T(4,128)}, u32[]{:S(2)}) copy-start(f32[4,128]{1,0:T(4,128)} %param.17) | copy-start | bytes 6148
  155.0 1.2 copy-start
  172.2 9.0 %copy-start.7 = (f32[40,128]{1,0:T(8,128)S(1)}, f32[40,128]{1,0:T(8,128)}, u32[]{:S(2)}) copy-start(f32[40,128]{1,0:T(8,128)} %param.14) | copy-start | bytes 61444
  173.7 7.9 %copy-start.4 = (f32[128,40,40]{0,2,1:T(8,128)}, f32[128,40,40]{0,2,1:T(8,128)S(1)}, u32[]{:S(2)}) copy-start(f32[128,40,40]{0,2,1:T(8,128)S(1)} %copy.63) | copy-start | bytes 2457604
  176.7 24.4 %all-to-all-start.2 = ((bf16[4,40,40,128]{3,2,1,0:T(8,128)(2,1)}), bf16[4,40,40,128]{3,2,1,0:T(8,128)(2,1)S(1)}, u32[]{:S(2)}, u32[]{:S(2)}) async-start(bf16[4,40,40,128]{3,2,1,0:T(8,128)(2,1)} %broadcast_in_dim.45), calls=%async_computation.2 | async-start | bytes 3276800 | tf_op jit(solution)/shard_map/all_to_all | solution.py:115
  333.6 1.2 copy-start.5

commit v3 on v2

--- a/solution.py
+++ b/solution.py
@@ -6,6 +6,7 @@
 from jax.experimental import pallas as pl
 from jax.experimental.pallas import tpu as pltpu
 from jax.sharding import PartitionSpec as P
+
 
 VMEM = pl.BlockSpec(memory_space=pltpu.VMEM)
 SMEM = pl.BlockSpec(memory_space=pltpu.SMEM)
@@ -120,24 +121,20 @@
     return lax.ppermute(x, axis, [(n, (n + step) % count) for n in range(count)])
 
 
-def ring_copies(x, axis, step=1):
+def all_copies(x, axis, step=1):
     length = lax.axis_size(axis) // step
-    ahead, behind = [x], [x]
-    for n in range(length // 2):
-        ahead.append(shifted(ahead[-1], axis, step))
-        if n < length - 1 - length // 2:
-            behind.append(shifted(behind[-1], axis, -step))
-    return jnp.stack(ahead + behind[:0:-1])
-
-
-def chip_ring_copies(x, axis):
-    count = lax.axis_size(axis)
-    mine = ring_copies(x, axis, 2)
-    theirs = lax.ppermute(mine, axis, [(n, n ^ 1) for n in range(count)])
-    return jnp.concatenate([mine, theirs])
-
-
-def on_device(
+    order = sorted(range(1, length), key=lambda n: -min(n, length - n))
+    copies = {}
+    for n in order:
+        copies[n] = shifted(x, axis, n * step)
+    return [x] + [copies[n] for n in range(1, length)]
+
+
+def other_core(x, axis):
+    return lax.ppermute(x, axis, [(n, n ^ 1) for n in range(lax.axis_size(axis))])
+
+
+def whole_step(
     orbital_ints,
     occ_energy,
     pair_row,
@@ -158,14 +155,15 @@
     chunk = cap * cells // 128
     per_block = orbital_ints.shape[0]
 
-    payload, target = call(
+    make_requests = call(
         functools.partial(request_kernel, cap),
         [jax.ShapeDtypeStruct((groups, 128), F32), jax.ShapeDtypeStruct((links, pairs), I32)],
         [VMEM, VMEM, SMEM],
         flops=10**7,
         nbytes=10**5,
         many=True,
-    )(partner_owner[0].T, partner_slot[0].T, occ_energy)
+    )
+    payload, target = make_requests(partner_owner[0].T, partner_slot[0].T, occ_energy)
     incoming = lax.all_to_all(payload, ("row", "col"), split_axis=0, concat_axis=0, tiled=True)
 
     gather = call(
@@ -205,21 +203,27 @@
     def sum_over_fit(x):
         return from_everyone(x.astype(BF16), "fit").astype(F32).sum(axis=0)
 
-    outgoing, own_ints = lax.optimization_barrier((outgoing_tiles(amplitudes), orbital_ints))
+    outgoing, row_blocks, chip_blocks = lax.optimization_barrier(
+        (
+            outgoing_tiles(amplitudes),
+            all_copies(orbital_ints, "col"),
+            all_copies(orbital_ints, "row", 2),
+        )
+    )
     tiles = returned_tiles(outgoing)
-
-    row_ints = ring_copies(own_ints, "col").reshape(-1, *orbital_ints.shape[1:])
-    col_ints = chip_ring_copies(own_ints, "row").reshape(-1, *orbital_ints.shape[1:])
+    row_ints = jnp.concatenate(row_blocks)
+    core_ints = jnp.concatenate(chip_blocks)
+    col_ints = jnp.concatenate([core_ints, other_core(core_ints, "row")])
     owner_col, inner_row = pair_row // per_block, pair_row % per_block
     owner_row, inner_col = pair_col // per_block, pair_col % per_block
     my_row, my_col = lax.axis_index("row"), lax.axis_index("col")
     back = (my_col - owner_col) % cols
     chips_back = (my_row // 2 - owner_row // 2) % (rows // 2)
-    other_core = (my_row + owner_row) % 2
+    core_off = (my_row + owner_row) % 2
     kernel = jnp.einsum(
         "pax,pbx->abp",
         row_ints[back * per_block + inner_row],
-        col_ints[(other_core * (rows // 2) + chips_back) * per_block + inner_col],
+        col_ints[(core_off * (rows // 2) + chips_back) * per_block + inner_col],
         preferred_element_type=F32,
     )
     energies = incoming[:, cap : cap + per_block].reshape(rows, cols, per_block)
@@ -254,7 +258,7 @@
         P("fit", ("row", "col"), None),
     )
     return jax.shard_map(
-        on_device,
+        whole_step,
         mesh=mesh,
         in_specs=placed,
         out_specs=(P(None, None, ("row", "col")), P(None, None, ("row", "col"))),

time: 336 us -> 304 us (0.905)
  waiting for transfers between devices: 91.5 us -> 49.5 us
  local copies, waits for them, and re-layouts: 51.3 us -> 57.9 us
  starting transfers between devices: 36.2 us -> 42.6 us
  blocking collectives: 111 us -> 107 us
    ppermute x10, waiting for transfers between devices: 64.6 us -> 0.03 us  [shifted(): lax.ppermute(x, axis, [(n, (n + step) % count) for n in range(count)])]
    all_to_all x1, waiting for transfers between devices: 0.01 us -> 28.9 us  [returned_tiles(): lax.all_to_all(outgoing, ('row', 'col'), split_axis=0, concat_axis=0, til...]
    ppermute x10, starting transfers between devices: 14.4 us -> 23 us  [shifted(): lax.ppermute(x, axis, [(n, (n + step) % count) for n in range(count)])]
    all_to_all x1, waiting for transfers between devices: 7.37 us -> 0.01 us  [whole_step(): lax.all_to_all(payload, ('row', 'col'), split_axis=0, concat_axis=0, tile...]
    unnamed x34 -> x52, local copies, waits for them, and re-layouts: 18.4 us -> 25.7 us
    all_to_all x1, blocking collectives: 86.9 us -> 83 us  [returned_tiles(): lax.all_to_all(outgoing, ('row', 'col'), split_axis=0, concat_axis=0, til...]
  transfers between devices with their start and end apart: 14 -> 14, of which waited for: 6 -> 2; matrix products, arithmetic and copies ran while one was open for 13% -> 16% of each run, Pallas kernels for 0% -> 2%
where the time goes in v3:
time: 304 us; the launch traced here: 303 us
  blocking collectives  107 us (35%)
  local copies, waits for them, and re-layouts  57.9 us (19%)
  waiting for transfers between devices  49.5 us (16%)
  starting transfers between devices  42.6 us (14%)
  matrix products  27.2 us (9%)
  Pallas kernels  10.2 us (3%)
  other arithmetic  7.95 us (3%)
    all_to_all x1, blocking collectives, returned_tiles(): lax.all_to_all(outgoing, ('row', 'col'), split_axis=0, concat_axis=0, til...  83 us
    all_to_all x1, waiting for transfers between devices, returned_tiles(): lax.all_to_all(outgoing, ('row', 'col'), split_axis=0, concat_axis=0, til...  28.9 us
    unnamed x52, local copies, waits for them, and re-layouts  25.7 us
    all_to_all x1, blocking collectives, from_everyone(): return lax.all_to_all(copies, axis, split_axis=0, concat_axis=0, tiled=True)  23.8 us
    ppermute x10, starting transfers between devices, shifted(): lax.ppermute(x, axis, [(n, (n + step) % count) for n in range(count)])  23 us
    all_to_all x1, waiting for transfers between devices, from_everyone(): return lax.all_to_all(copies, axis, split_axis=0, concat_axis=0, tiled=True)  20.6 us
    dot_general x2, matrix products, coupling_of(): jnp.einsum('adcp,edcp->aecp', half_product, intersections, preferred_elem...  18.8 us
    reshape x2, local copies, waits for them, and re-layouts, returned_tiles(): return select(target, returned).reshape(links, size, size, pairs)  11.5 us
  transfers between devices with their start and end apart: 14, of which 2 were waited for; matrix products, arithmetic and copies ran while one was open for 16% of the time, Pallas kernels for 2%

profile of v3, /device:TPU:32, one launch (start us, length us, event | category | flops | bytes accessed | tf_op | source)
XLA Modules:
  0.0 303.1 jit_solution(14450018043283133586)
XLA Ops:
  0.6 2.0 collective-permute-start
  2.6 4.5 %collective-permute-start.1 = (bf16[2,40,640]{2,1,0:T(8,128)(2,1)}, bf16[2,40,640]{2,1,0:T(8,128)(2,1)S(1)}, u32[]{:S(2)}, u32[]{:S(2)}) collective-permute-start(bf16[2,40,640]{2,1,0:T(8,128)(2,1)} %param.10), channel_id=1, source_target_pairs={{0,8},{4,12},{8,16},{12,20},{16,24},{20,28},{24,0},{28,4},{1,9},{5... | collective-permute-start | bytes 307208 | tf_op jit(solution)/shard_map/ppermute | solution.py:121
  7.1 1.9 collective-permute-start.2
  10.5 3.1 %collective-permute-start.4 = (bf16[2,40,640]{2,1,0:T(8,128)(2,1)}, bf16[2,40,640]{2,1,0:T(8,128)(2,1)S(1)}, u32[]{:S(2)}, u32[]{:S(2)}) collective-permute-start(bf16[2,40,640]{2,1,0:T(8,128)(2,1)} %param.10), channel_id=1, source_target_pairs={{0,20},{4,24},{8,28},{12,0},{16,4},{20,8},{24,12},{28,16},{1,21},{... | collective-permute-start | bytes 307208 | tf_op jit(solution)/shard_map/ppermute | solution.py:121
  15.6 1.7 shard_map.113
  17.3 9.3 %all-to-all-start = ((f32[64,1,128]{2,1,0:T(1,128)}), f32[64,1,128]{2,1,0:T(1,128)S(1)}, u32[]{:S(2)}, u32[]{:S(2)}) async-start(f32[64,1,128]{2,1,0:T(1,128)} %bitcast.5), calls=%async_computation | async-start | bytes 65536 | tf_op jit(solution)/shard_map/all_to_all | solution.py:167
  26.7 2.8 collective-permute-start.5
  32.4 2.9 collective-permute-start.8
  38.0 3.0 %shard_map.114 = bf16[64,200,128]{2,1,0:T(8,128)(2,1)} custom-call(f32[64,128]{1,0:T(8,128)S(1)} %bitcast.55, bf16[1600,128]{1,0:T(8,128)(2,1)S(1)} %bitcast.52), custom_call_target="tpu_custom_call" | custom-call | flops 419430400 | bytes 3276800 | tf_op jit(solution)/shard_map/pallas_call | solution.py:192
  41.8 5.6 %all-to-all-start.1 = ((bf16[64,200,128]{2,1,0:T(8,128)(2,1)}), bf16[64,200,128]{2,1,0:T(8,128)(2,1)S(1)}, u32[]{:S(2)}, u32[]{:S(2)}) async-start(bf16[64,200,128]{2,1,0:T(8,128)(2,1)} %shard_map.114), calls=%async_computation.1 | async-start | bytes 6553600 | tf_op jit(solution)/shard_map/all_to_all | solution.py:186
  47.5 6.5 %copy.60 = bf16[40,40,4,128]{1,0,3,2:T(8,128)(2,1)} copy(bf16[40,40,4,128]{3,2,1,0:T(4,128)(2,1)} %param.16) | data formatting | bytes 3276800 | tf_op args[6]
  54.1 1.8 pad_maximum_fusion
  69.7 1.6 constant_dynamic-update-slice_fusion.1
  71.3 5.3 %gather_fusion.1 = bf16[128,40,640]{2,1,0:T(8,128)(2,1)} fusion(bf16[16,40,640]{2,1,0:T(8,128)(2,1)} %get-tuple-element.33, s32[1024]{0:T(1024)S(1)} %get-tuple-element.34), kind=kCustom, calls=%fused_computation.1 | custom fusion | bytes 13107712 | tf_op jit(solution)/shard_map/gather | solution.py:225
  76.5 1.8 constant_dynamic-update-slice_fusion
  78.3 5.3 %gather_fusion = bf16[128,40,640]{2,1,0:T(8,128)(2,1)} fusion(bf16[16,40,640]{2,1,0:T(8,128)(2,1)} %constant_dynamic-update-slice_fusion, s32[1024]{0:T(1024)S(1)} %get-tuple-element.35), kind=kCustom, calls=%fused_computation | custom fusion | bytes 13107712 | tf_op jit(solution)/shard_map/gather | solution.py:226
  83.6 8.5 %fusion.26 = f32[128,40,40]{2,1,0:T(8,128)} fusion(bf16[128,40,640]{2,1,0:T(8,128)(2,1)} %gather_fusion, bf16[128,40,640]{2,1,0:T(8,128)(2,1)} %gather_fusion.1), kind=kOutput, calls=%fused_computation.79 | convolution fusion | flops 262144000 | bytes 13926400 | tf_op jit(solution)/shard_map/pax,pbx->abp/dot_general | solution.py:223
  92.1 3.1 %copy.64 = f32[128,40,40]{0,1,2:T(8,128)} copy(f32[128,40,40]{2,1,0:T(8,128)} %fusion.26) | data formatting | bytes 1638400 | tf_op jit(solution)/shard_map/pax,pbx->abp/dot_general | solution.py:223
  95.1 28.9 %all-to-all-done.1.back_ref = bf16[64,200,128]{2,1,0:T(8,128)(2,1)S(1)} async-done(((bf16[64,200,128]{2,1,0:T(8,128)(2,1)}), bf16[64,200,128]{2,1,0:T(8,128)(2,1)S(1)}, u32[]{:S(2)}, u32[]{:S(2)}) %all-to-all-start.1) | async-done | bytes 3276832 | tf_op jit(solution)/shard_map/all_to_all | solution.py:186
  124.1 2.1 shard_map.115
  127.3 6.6 %copy.59 = bf16[4,40,40,128]{1,2,3,0:T(8,128)(2,1)} copy(bf16[4,40,40,128]{3,2,1,0:T(8,128)(2,1)} %bitcast.54) | data formatting | bytes 3276800 | tf_op jit(solution)/shard_map/reshape | solution.py:189
  133.9 9.4 %multiply_reduce_fusion.1 = f32[128,40,40]{2,1,0:T(8,128)S(1)} fusion(f32[4,128]{1,0:T(4,128)S(1)} %copy-done.10, bf16[40,40,4,128]{1,0,3,2:T(8,128)(2,1)} %copy.60, bf16[4,40,40,128]{1,2,3,0:T(8,128)(2,1)} %copy.59), kind=kOutput, calls=%fused_computation.3 | convolution fusion | flops 133324800 | bytes 4098048 | tf_op jit(solution)/shard_map/adcp,edcp->aecp/dot_general | solution.py:198
  143.3 1.6 copy.63
  144.9 1.6 fusion.17
  147.8 4.5 %all-to-all-start.2 = ((bf16[4,40,40,128]{3,2,1,0:T(8,128)(2,1)}), bf16[4,40,40,128]{3,2,1,0:T(8,128)(2,1)S(1)}, u32[]{:S(2)}, u32[]{:S(2)}) async-start(bf16[4,40,40,128]{3,2,1,0:T(8,128)(2,1)} %broadcast_in_dim.45), calls=%async_computation.2 | async-start | bytes 3276800 | tf_op jit(solution)/shard_map/all_to_all | solution.py:116
  152.7 20.6 %all-to-all-done.2 = bf16[4,40,40,128]{3,2,1,0:T(8,128)(2,1)S(1)} async-done(((bf16[4,40,40,128]{3,2,1,0:T(8,128)(2,1)}), bf16[4,40,40,128]{3,2,1,0:T(8,128)(2,1)S(1)}, u32[]{:S(2)}, u32[]{:S(2)}) %all-to-all-start.2) | async-done | bytes 1638432 | tf_op jit(solution)/shard_map/all_to_all | solution.py:116
  175.0 83.0 %all_to_all.31.back_ref = bf16[64,200,128]{2,1,0:T(8,128)(2,1)S(1)} all-to-all(bf16[64,200,128]{2,1,0:T(8,128)(2,1)S(1)} %shard_map.116), channel_id=1, replica_groups=mesh['row'=8,'col'=8,'fit'=4] {'row','col'}, dimensions={0} | all-to-all | bytes 6553600 | tf_op jit(solution)/shard_map/all_to_all | solution.py:186
  258.0 2.1 shard_map.117
  260.1 4.9 %copy.68 = bf16[4,40,40,128]{1,2,3,0:T(8,128)(2,1)} copy(bf16[4,40,40,128]{3,2,1,0:T(8,128)(2,1)S(1)} %bitcast.53) | data formatting | bytes 3276800 | tf_op jit(solution)/shard_map/reshape | solution.py:189
  265.0 9.4 %multiply_reduce_fusion = f32[128,40,40]{2,1,0:T(8,128)S(1)} fusion(f32[4,128]{1,0:T(4,128)S(1)} %copy-done.10, bf16[40,40,4,128]{1,0,3,2:T(8,128)(2,1)} %copy.60, bf16[4,40,40,128]{1,2,3,0:T(8,128)(2,1)} %copy.68), kind=kOutput, calls=%fused_computation.2 | convolution fusion | flops 133324800 | bytes 4098048 | tf_op jit(solution)/shard_map/adcp,edcp->aecp/dot_general | solution.py:198
  274.4 1.8 copy.72
  277.9 23.8 %all_to_all.32 = bf16[4,40,40,128]{3,2,1,0:T(8,128)(2,1)S(1)} all-to-all(bf16[4,40,40,128]{3,2,1,0:T(8,128)(2,1)S(1)} %broadcast_in_dim.51), channel_id=1, replica_groups=mesh['row'=8,'col'=8,'fit'=4] {'fit'}, dimensions={0} | all-to-all | bytes 3276800 | tf_op jit(solution)/shard_map/all_to_all | solution.py:116
  (87 shorter events, 31.4 us)
Async XLA Ops:
  0.6 26.0 %collective-permute-start = (bf16[2,40,640]{2,1,0:T(8,128)(2,1)}, bf16[2,40,640]{2,1,0:T(8,128)(2,1)S(1)}, u32[]{:S(2)}, u32[]{:S(2)}) collective-permute-start(bf16[2,40,640]{2,1,0:T(8,128)(2,1)} %param.10), channel_id=1, source_target_pairs={{0,4},{4,8},{8,12},{12,16},{16,20},{20,24},{24,28},{28,0},{1,5},{5... | collective-permute-start | bytes 307208 | tf_op jit(solution)/shard_map/ppermute | solution.py:121
  2.6 26.8 %collective-permute-start.1 = (bf16[2,40,640]{2,1,0:T(8,128)(2,1)}, bf16[2,40,640]{2,1,0:T(8,128)(2,1)S(1)}, u32[]{:S(2)}, u32[]{:S(2)}) collective-permute-start(bf16[2,40,640]{2,1,0:T(8,128)(2,1)} %param.10), channel_id=1, source_target_pairs={{0,8},{4,12},{8,16},{12,20},{16,24},{20,28},{24,0},{28,4},{1,9},{5... | collective-permute-start | bytes 307208 | tf_op jit(solution)/shard_map/ppermute | solution.py:121
  7.1 23.8 %collective-permute-start.2 = (bf16[2,40,640]{2,1,0:T(8,128)(2,1)}, bf16[2,40,640]{2,1,0:T(8,128)(2,1)S(1)}, u32[]{:S(2)}, u32[]{:S(2)}) collective-permute-start(bf16[2,40,640]{2,1,0:T(8,128)(2,1)} %param.10), channel_id=1, source_target_pairs={{0,12},{4,16},{8,20},{12,24},{16,28},{20,0},{24,4},{28,8},{1,13},{... | collective-permute-start | bytes 307208 | tf_op jit(solution)/shard_map/ppermute | solution.py:121
  9.0 23.4 %collective-permute-start.3 = (bf16[2,40,640]{2,1,0:T(8,128)(2,1)}, bf16[2,40,640]{2,1,0:T(8,128)(2,1)S(1)}, u32[]{:S(2)}, u32[]{:S(2)}) collective-permute-start(bf16[2,40,640]{2,1,0:T(8,128)(2,1)} %param.10), channel_id=1, source_target_pairs={{0,16},{4,20},{8,24},{12,28},{16,0},{20,4},{24,8},{28,12},{1,17},{... | collective-permute-start | bytes 307208 | tf_op jit(solution)/shard_map/ppermute | solution.py:121
  10.5 24.8 %collective-permute-start.4 = (bf16[2,40,640]{2,1,0:T(8,128)(2,1)}, bf16[2,40,640]{2,1,0:T(8,128)(2,1)S(1)}, u32[]{:S(2)}, u32[]{:S(2)}) collective-permute-start(bf16[2,40,640]{2,1,0:T(8,128)(2,1)} %param.10), channel_id=1, source_target_pairs={{0,20},{4,24},{8,28},{12,0},{16,4},{20,8},{24,12},{28,16},{1,21},{... | collective-permute-start | bytes 307208 | tf_op jit(solution)/shard_map/ppermute | solution.py:121
  13.6 0.7 copy-start.1
  14.3 0.7 copy-start.2
  17.3 20.7 %all-to-all-start = ((f32[64,1,128]{2,1,0:T(1,128)}), f32[64,1,128]{2,1,0:T(1,128)S(1)}, u32[]{:S(2)}, u32[]{:S(2)}) async-start(f32[64,1,128]{2,1,0:T(1,128)} %bitcast.5), calls=%async_computation | async-start | bytes 65536 | tf_op jit(solution)/shard_map/all_to_all | solution.py:167
  26.7 8.6 %copy-start.11 = (bf16[2,40,640]{2,1,0:T(8,128)(2,1)}, bf16[2,40,640]{2,1,0:T(8,128)(2,1)S(1)}, u32[]{:S(2)}) copy-start(bf16[2,40,640]{2,1,0:T(8,128)(2,1)S(1)} %collective-permute-done) | copy-start | bytes 307204
  26.7 14.4 %collective-permute-start.5 = (bf16[2,40,640]{2,1,0:T(8,128)(2,1)}, bf16[2,40,640]{2,1,0:T(8,128)(2,1)S(1)}, u32[]{:S(2)}, u32[]{:S(2)}) collective-permute-start(bf16[2,40,640]{2,1,0:T(8,128)(2,1)} %param.10), channel_id=1, source_target_pairs={{0,24},{4,28},{8,0},{12,4},{16,8},{20,12},{24,16},{28,20},{1,25},{... | collective-permute-start | bytes 307208 | tf_op jit(solution)/shard_map/ppermute | solution.py:121
  29.4 5.9 %copy-start.12 = (bf16[2,40,640]{2,1,0:T(8,128)(2,1)}, bf16[2,40,640]{2,1,0:T(8,128)(2,1)S(1)}, u32[]{:S(2)}) copy-start(bf16[2,40,640]{2,1,0:T(8,128)(2,1)S(1)} %collective-permute-done.1) | copy-start | bytes 307204
  29.4 11.6 %collective-permute-start.6 = (bf16[2,40,640]{2,1,0:T(8,128)(2,1)}, bf16[2,40,640]{2,1,0:T(8,128)(2,1)S(1)}, u32[]{:S(2)}, u32[]{:S(2)}) collective-permute-start(bf16[2,40,640]{2,1,0:T(8,128)(2,1)} %param.10), channel_id=1, source_target_pairs={{0,28},{4,0},{8,4},{12,8},{16,12},{20,16},{24,20},{28,24},{1,29},{... | collective-permute-start | bytes 307208 | tf_op jit(solution)/shard_map/ppermute | solution.py:121
  30.9 4.4 %copy-start.13 = (bf16[2,40,640]{2,1,0:T(8,128)(2,1)}, bf16[2,40,640]{2,1,0:T(8,128)(2,1)S(1)}, u32[]{:S(2)}) copy-start(bf16[2,40,640]{2,1,0:T(8,128)(2,1)S(1)} %collective-permute-done.2) | copy-start | bytes 307204
  30.9 10.2 %collective-permute-start.7 = (bf16[2,40,640]{2,1,0:T(8,128)(2,1)}, bf16[2,40,640]{2,1,0:T(8,128)(2,1)S(1)}, u32[]{:S(2)}, u32[]{:S(2)}) collective-permute-start(bf16[2,40,640]{2,1,0:T(8,128)(2,1)} %param.10), channel_id=1, source_target_pairs={{0,64},{32,96},{64,128},{96,160},{128,192},{160,224},{192,0},{224,... | collective-permute-start | bytes 307208 | tf_op jit(solution)/shard_map/ppermute | solution.py:121
  32.4 2.9 copy-start.14
  32.4 8.7 %collective-permute-start.8 = (bf16[2,40,640]{2,1,0:T(8,128)(2,1)}, bf16[2,40,640]{2,1,0:T(8,128)(2,1)S(1)}, u32[]{:S(2)}, u32[]{:S(2)}) collective-permute-start(bf16[2,40,640]{2,1,0:T(8,128)(2,1)} %param.10), channel_id=1, source_target_pairs={{0,128},{32,160},{64,192},{96,224},{128,0},{160,32},{192,64},{224,... | collective-permute-start | bytes 307208 | tf_op jit(solution)/shard_map/ppermute | solution.py:121
  35.3 5.8 %copy-start.15 = (bf16[2,40,640]{2,1,0:T(8,128)(2,1)}, bf16[2,40,640]{2,1,0:T(8,128)(2,1)S(1)}, u32[]{:S(2)}) copy-start(bf16[2,40,640]{2,1,0:T(8,128)(2,1)S(1)} %collective-permute-done.4) | copy-start | bytes 307204
  35.3 5.8 %collective-permute-start.9 = (bf16[2,40,640]{2,1,0:T(8,128)(2,1)}, bf16[2,40,640]{2,1,0:T(8,128)(2,1)S(1)}, u32[]{:S(2)}, u32[]{:S(2)}) collective-permute-start(bf16[2,40,640]{2,1,0:T(8,128)(2,1)} %param.10), channel_id=1, source_target_pairs={{0,192},{32,224},{64,0},{96,32},{128,64},{160,96},{192,128},{224,1... | collective-permute-start | bytes 307208 | tf_op jit(solution)/shard_map/ppermute | solution.py:121
  41.0 13.0 %copy-start.18 = (s32[128]{0:T(128)S(1)}, s32[128]{0:T(128)}, u32[]{:S(2)}) copy-start(s32[128]{0:T(128)} %param.13) | copy-start | bytes 1540
  41.0 13.0 %copy-start.19 = (s32[128]{0:T(128)S(1)}, s32[128]{0:T(128)}, u32[]{:S(2)}) copy-start(s32[128]{0:T(128)} %param.12) | copy-start | bytes 1540
  41.0 13.0 %copy-start.6 = (bf16[2,40,640]{2,1,0:T(8,128)(2,1)S(1)}, bf16[2,40,640]{2,1,0:T(8,128)(2,1)}, u32[]{:S(2)}) copy-start(bf16[2,40,640]{2,1,0:T(8,128)(2,1)} %param.10) | copy-start | bytes 307204
  41.1 0.7 copy-start.17
  41.1 0.7 copy-start.7
  41.1 0.7 copy-start.8
  41.8 82.2 %all-to-all-start.1 = ((bf16[64,200,128]{2,1,0:T(8,128)(2,1)}), bf16[64,200,128]{2,1,0:T(8,128)(2,1)S(1)}, u32[]{:S(2)}, u32[]{:S(2)}) async-start(bf16[64,200,128]{2,1,0:T(8,128)(2,1)} %shard_map.114), calls=%async_computation.1 | async-start | bytes 6553600 | tf_op jit(solution)/shard_map/all_to_all | solution.py:186
  55.9 20.7 %collective-permute-start.10 = (bf16[8,40,640]{2,1,0:T(8,128)(2,1)}, bf16[8,40,640]{2,1,0:T(8,128)(2,1)}, u32[]{:S(2)}, u32[]{:S(2)}) collective-permute-start(bf16[8,40,640]{2,1,0:T(8,128)(2,1)} %pad_maximum_fusion), channel_id=1, source_target_pairs={{0,32},{32,0},{64,96},{96,64},{128,160},{160,128},{192,224},{224,1... | collective-permute-start | bytes 1228808 | tf_op jit(solution)/shard_map/ppermute | solution.py:134
  124.1 9.8 %copy-start.10 = (f32[4,128]{1,0:T(4,128)S(1)}, f32[4,128]{1,0:T(4,128)}, u32[]{:S(2)}) copy-start(f32[4,128]{1,0:T(4,128)} %param.17) | copy-start | bytes 6148
  126.1 1.2 copy-start
  143.3 9.0 %copy-start.9 = (f32[40,128]{1,0:T(8,128)S(1)}, f32[40,128]{1,0:T(8,128)}, u32[]{:S(2)}) copy-start(f32[40,128]{1,0:T(8,128)} %param.14) | copy-start | bytes 61444
  144.9 7.9 %copy-start.4 = (f32[128,40,40]{0,2,1:T(8,128)}, f32[128,40,40]{0,2,1:T(8,128)S(1)}, u32[]{:S(2)}) copy-start(f32[128,40,40]{0,2,1:T(8,128)S(1)} %copy.63) | copy-start | bytes 2457604
  147.8 25.5 %all-to-all-start.2 = ((bf16[4,40,40,128]{3,2,1,0:T(8,128)(2,1)}), bf16[4,40,40,128]{3,2,1,0:T(8,128)(2,1)S(1)}, u32[]{:S(2)}, u32[]{:S(2)}) async-start(bf16[4,40,40,128]{3,2,1,0:T(8,128)(2,1)} %broadcast_in_dim.45), calls=%async_computation.2 | async-start | bytes 3276800 | tf_op jit(solution)/shard_map/all_to_all | solution.py:116
  301.9 1.2 copy-start.5
  (2 other events, 1.3 us)

commit v4 on v3

--- a/solution.py
+++ b/solution.py
@@ -56,11 +56,26 @@
     low_hits, high_hits = low[...], high[...]
     hits = jnp.concatenate([low_hits, high_hits], axis=1).reshape(groups * cap, pairs).astype(BF16)
     whole = cells // 128
-    for n in range(whole):
-        block = lax.dot_general(
+
+    def some_blocks(turn, carry):
+        for m in range(3):
+            n = turn * 3 + m
+            block = lax.dot_general(
+                hits,
+                sent_ref[pl.ds(pl.multiple_of(n * 128, 128), 128), :],
+                NT,
+                preferred_element_type=F32,
+            )
+            here = pl.ds(pl.multiple_of(n * cap, cap), cap)
+            out_ref[:, here, :] = block.astype(BF16).reshape(groups, cap, 128)
+        return carry
+
+    lax.fori_loop(0, whole // 3, some_blocks, 0)
+    for n in range(whole // 3 * 3, whole):
+        some = lax.dot_general(
             hits, sent_ref[n * 128 : (n + 1) * 128, :], NT, preferred_element_type=F32
         )
-        out_ref[:, n * cap : (n + 1) * cap, :] = block.astype(BF16).reshape(groups, cap, 128)
+        out_ref[:, n * cap : (n + 1) * cap, :] = some.astype(BF16).reshape(groups, cap, 128)
     rest = sent_ref[whole * 128 :, :]
     none = jnp.zeros((128 - rest.shape[0], pairs), BF16)
     low_hits = low_hits.reshape(groups * half, pairs).astype(BF16)
@@ -99,6 +114,30 @@
         out_ref[k, whole * 128 :, :] = block[:, k * pairs : (k + 1) * pairs]
 
 
+def stacked_kernel(*refs):
+    *blocks, out_ref = refs
+    count = blocks[0].shape[0]
+    for n, block in enumerate(blocks):
+        out_ref[n * count : (n + 1) * count] = block[...]
+
+
+def rounded_kernel(x_ref, y_ref, low_ref, high_ref):
+    half = low_ref.shape[0]
+    low_ref[...] = (x_ref[:half] - y_ref[:half]).astype(BF16)
+    high_ref[...] = (x_ref[half:] - y_ref[half:]).astype(BF16)
+
+
+def added_kernel(low_ref, high_ref, low_there, high_there, low_out, high_out):
+    low_out[...] = (low_ref[...].astype(F32) + low_there[...].astype(F32)).astype(BF16)
+    high_out[...] = (high_ref[...].astype(F32) + high_there[...].astype(F32)).astype(BF16)
+
+
+def joined_kernel(low_ref, high_ref, low_there, high_there, out_ref):
+    half = low_ref.shape[0]
+    out_ref[:half] = low_ref[...].astype(F32) + low_there[...].astype(F32)
+    out_ref[half:] = high_ref[...].astype(F32) + high_there[...].astype(F32)
+
+
 def call(kernel, out_shape, in_specs, scratch=(), flops=0, nbytes=0, many=False):
     return pl.pallas_call(
         kernel,
@@ -111,9 +150,10 @@
     )
 
 
-def from_everyone(x, axis):
-    copies = jnp.broadcast_to(x, (lax.axis_size(axis), *x.shape))
-    return lax.all_to_all(copies, axis, split_axis=0, concat_axis=0, tiled=True)
+def stacked(blocks):
+    first, *shape = blocks[0].shape
+    whole = jax.ShapeDtypeStruct((len(blocks) * first, *shape), blocks[0].dtype)
+    return call(stacked_kernel, whole, [VMEM] * len(blocks), nbytes=2 * 10**6)(*blocks)
 
 
 def shifted(x, axis, step):
@@ -200,8 +240,23 @@
         )
         return jnp.sum(coupled * coupling_fock[None, None, :, :], axis=2)
 
-    def sum_over_fit(x):
-        return from_everyone(x.astype(BF16), "fit").astype(F32).sum(axis=0)
+    def sum_over_fit(x, y):
+        count = lax.axis_size("fit")
+        sides = [(n, n ^ 1) for n in range(count)], [(n, count - 1 - n) for n in range(count)]
+        part = jax.ShapeDtypeStruct((cells // 2, pairs), BF16)
+        halves = call(rounded_kernel, [part] * 2, [VMEM] * 2, nbytes=10**6, many=True)(
+            x.reshape(cells, pairs), y.reshape(cells, pairs)
+        )
+        for turn in range(2):
+            there = [lax.ppermute(h, "fit", sides[n ^ turn]) for n, h in enumerate(halves)]
+            if turn == 0:
+                halves = call(added_kernel, [part] * 2, [VMEM] * 4, nbytes=10**6, many=True)(
+                    *halves, *there
+                )
+        whole = jax.ShapeDtypeStruct((cells, pairs), F32)
+        return call(joined_kernel, whole, [VMEM] * 4, nbytes=10**6)(*halves, *there).reshape(
+            size, size, pairs
+        )
 
     outgoing, row_blocks, chip_blocks = lax.optimization_barrier(
         (
@@ -211,9 +266,9 @@
         )
     )
     tiles = returned_tiles(outgoing)
-    row_ints = jnp.concatenate(row_blocks)
-    core_ints = jnp.concatenate(chip_blocks)
-    col_ints = jnp.concatenate([core_ints, other_core(core_ints, "row")])
+    row_ints = stacked(row_blocks)
+    core_ints = stacked(chip_blocks)
+    col_ints = stacked([core_ints, other_core(core_ints, "row")])
     owner_col, inner_row = pair_row // per_block, pair_row % per_block
     owner_row, inner_col = pair_col // per_block, pair_col % per_block
     my_row, my_col = lax.axis_index("row"), lax.axis_index("col")
@@ -238,9 +293,9 @@
     denominator = virt_energy[:, None, :] + virt_energy[None, :, :] - occupied[None, None, :]
 
     first = coupling_of(tiles)
-    current = sum_over_fit(first - kernel) / denominator
+    current = sum_over_fit(first, kernel) / denominator
     second = coupling_of(returned_tiles(outgoing_tiles(current)))
-    residual = sum_over_fit(first - second)
+    residual = sum_over_fit(first, second)
     return (current - residual / denominator, residual)
 
 

time: 304 us -> 291 us (0.957)
  blocking collectives: 107 us -> 83.9 us
  local copies, waits for them, and re-layouts: 57.9 us -> 35.2 us
  waiting for transfers between devices: 49.5 us -> 71.6 us
  starting transfers between devices: 42.6 us -> 48.5 us
  Pallas kernels: 10.2 us -> 15.3 us
  other arithmetic: 7.95 us -> 4.68 us
    all_to_all x1 -> x0, blocking collectives: 23.8 us -> none  [from_everyone(): return lax.all_to_all(copies, axis, split_axis=0, concat_axis=0, tiled=True)]
    ppermute x0 -> x8, waiting for transfers between devices: none -> 22.5 us  [sum_over_fit(): lax.ppermute(h, 'fit', sides[n ^ turn])]
    all_to_all x1 -> x0, waiting for transfers between devices: 20.6 us -> none  [from_everyone(): return lax.all_to_all(copies, axis, split_axis=0, concat_axis=0, tiled=True)]
    all_to_all x1, waiting for transfers between devices: 28.9 us -> 49.1 us  [returned_tiles(): lax.all_to_all(outgoing, ('row', 'col'), split_axis=0, concat_axis=0, til...]
    unnamed x52 -> x19, local copies, waits for them, and re-layouts: 25.7 us -> 8.56 us
    ppermute x0 -> x8, starting transfers between devices: none -> 9.38 us  [sum_over_fit(): lax.ppermute(h, 'fit', sides[n ^ turn])]
    all_to_all x1 -> x0, starting transfers between devices: 4.47 us -> none  [from_everyone(): return lax.all_to_all(copies, axis, split_axis=0, concat_axis=0, tiled=True)]
    dot_general x1 -> x0, local copies, waits for them, and re-layouts: 3.05 us -> none  [whole_step(): jnp.einsum('pax,pbx->abp', row_ints[back * per_block + inner_row], col_in...]
  transfers between devices with their start and end apart: 14 -> 21, of which waited for: 2 -> 9; matrix products, arithmetic and copies ran while one was open for 16% -> 10% of each run, Pallas kernels for 2% -> 2%
where the time goes in v4:
time: 291 us; the launch traced here: 290 us
  blocking collectives  83.9 us (29%)
  waiting for transfers between devices  71.6 us (25%)
  starting transfers between devices  48.5 us (17%)
  local copies, waits for them, and re-layouts  35.2 us (12%)
  matrix products  30.2 us (10%)
  Pallas kernels  15.3 us (5%)
  other arithmetic  4.68 us (2%)
    all_to_all x1, blocking collectives, returned_tiles(): lax.all_to_all(outgoing, ('row', 'col'), split_axis=0, concat_axis=0, til...  83.9 us
    all_to_all x1, waiting for transfers between devices, returned_tiles(): lax.all_to_all(outgoing, ('row', 'col'), split_axis=0, concat_axis=0, til...  49.1 us
    ppermute x10, starting transfers between devices, shifted(): lax.ppermute(x, axis, [(n, (n + step) % count) for n in range(count)])  22.9 us
    ppermute x8, waiting for transfers between devices, sum_over_fit(): lax.ppermute(h, 'fit', sides[n ^ turn])  22.5 us
    dot_general x2, matrix products, coupling_of(): jnp.einsum('adcp,edcp->aecp', half_product, intersections, preferred_elem...  21.7 us
    reshape x2, local copies, waits for them, and re-layouts, returned_tiles(): return select(target, returned).reshape(links, size, size, pairs)  10 us
    ppermute x8, starting transfers between devices, sum_over_fit(): lax.ppermute(h, 'fit', sides[n ^ turn])  9.38 us
    all_to_all x1, starting transfers between devices, whole_step(): lax.all_to_all(payload, ('row', 'col'), split_axis=0, concat_axis=0, tile...  9.33 us
  transfers between devices with their start and end apart: 21, of which 9 were waited for; matrix products, arithmetic and copies ran while one was open for 10% of the time, Pallas kernels for 2%

profile of v4, /device:TPU:32, one launch (start us, length us, event | category | flops | bytes accessed | tf_op | source)
XLA Modules:
  0.0 290.3 jit_solution(4029342231850263144)
XLA Ops:
  0.6 2.0 collective-permute-start
  2.6 4.5 %collective-permute-start.1 = (bf16[2,40,640]{2,1,0:T(8,128)(2,1)}, bf16[2,40,640]{2,1,0:T(8,128)(2,1)S(1)}, u32[]{:S(2)}, u32[]{:S(2)}) collective-permute-start(bf16[2,40,640]{2,1,0:T(8,128)(2,1)} %refs_0_.1), channel_id=1, source_target_pairs={{0,8},{4,12},{8,16},{12,20},{16,24},{20,28},{24,0},{28,4},{1,9},{5... | collective-permute-start | bytes 307208 | tf_op jit(solution)/shard_map/ppermute | solution.py:161
  10.5 3.1 %collective-permute-start.4 = (bf16[2,40,640]{2,1,0:T(8,128)(2,1)}, bf16[2,40,640]{2,1,0:T(8,128)(2,1)S(1)}, u32[]{:S(2)}, u32[]{:S(2)}) collective-permute-start(bf16[2,40,640]{2,1,0:T(8,128)(2,1)} %refs_0_.1), channel_id=1, source_target_pairs={{0,20},{4,24},{8,28},{12,0},{16,4},{20,8},{24,12},{28,16},{1,21},{... | collective-permute-start | bytes 307208 | tf_op jit(solution)/shard_map/ppermute | solution.py:161
  17.3 9.3 %all-to-all-start = ((f32[64,1,128]{2,1,0:T(1,128)}), f32[64,1,128]{2,1,0:T(1,128)S(1)}, u32[]{:S(2)}, u32[]{:S(2)}) async-start(f32[64,1,128]{2,1,0:T(1,128)} %bitcast.5), calls=%async_computation | async-start | bytes 65536 | tf_op jit(solution)/shard_map/all_to_all | solution.py:207
  26.7 2.8 collective-permute-start.5
  32.4 2.9 collective-permute-start.8
  37.9 3.9 %shard_map.114 = bf16[64,200,128]{2,1,0:T(8,128)(2,1)} custom-call(f32[64,128]{1,0:T(8,128)S(1)} %bitcast.56, bf16[1600,128]{1,0:T(8,128)(2,1)S(1)} %bitcast.53), custom_call_target="tpu_custom_call" | custom-call | flops 419430400 | bytes 3276800 | tf_op jit(solution)/shard_map/pallas_call | solution.py:232
  41.8 6.4 %all-to-all-start.1 = ((bf16[64,200,128]{2,1,0:T(8,128)(2,1)}), bf16[64,200,128]{2,1,0:T(8,128)(2,1)}, u32[]{:S(2)}, u32[]{:S(2)}) async-start(bf16[64,200,128]{2,1,0:T(8,128)(2,1)} %shard_map.114), calls=%async_computation.1 | async-start | bytes 6553600 | tf_op jit(solution)/shard_map/all_to_all | solution.py:226
  48.8 6.5 %copy.41 = bf16[40,40,4,128]{1,0,3,2:T(8,128)(2,1)} copy(bf16[40,40,4,128]{3,2,1,0:T(4,128)(2,1)} %param.16) | data formatting | bytes 3276800 | tf_op args[6]
  56.4 4.2 %gather_fusion.1 = bf16[128,40,640]{2,1,0:T(8,128)(2,1)} fusion(bf16[16,40,640]{2,1,0:T(8,128)(2,1)S(1)} %shard_map.118, s32[1024]{0:T(1024)S(1)} %pad_clamp_fusion), kind=kCustom, calls=%fused_computation.1 | custom fusion | bytes 13107712 | tf_op jit(solution)/shard_map/gather | solution.py:280
  60.6 4.1 %gather_fusion = bf16[128,40,640]{2,1,0:T(8,128)(2,1)} fusion(bf16[16,40,640]{2,1,0:T(8,128)(2,1)S(1)} %shard_map.117, s32[1024]{0:T(1024)S(1)} %pad_clamp_fusion.1), kind=kCustom, calls=%fused_computation | custom fusion | bytes 13107712 | tf_op jit(solution)/shard_map/gather | solution.py:281
  64.7 8.5 %convolution_bitcast_fusion = f32[40,40,128]{0,1,2:T(8,128)} fusion(bf16[128,40,640]{2,1,0:T(8,128)(2,1)} %gather_fusion, bf16[128,40,640]{2,1,0:T(8,128)(2,1)} %gather_fusion.1), kind=kOutput, calls=%fused_computation.12 | convolution fusion | flops 262144000 | bytes 13926400 | tf_op jit(solution)/shard_map/pax,pbx->abp/dot_general | solution.py:278
  73.3 2.4 copy.45
  75.7 49.1 %all-to-all-done.1.back_ref = bf16[64,200,128]{2,1,0:T(8,128)(2,1)} async-done(((bf16[64,200,128]{2,1,0:T(8,128)(2,1)}), bf16[64,200,128]{2,1,0:T(8,128)(2,1)}, u32[]{:S(2)}, u32[]{:S(2)}) %all-to-all-start.1) | async-done | bytes 3276832 | tf_op jit(solution)/shard_map/all_to_all | solution.py:226
  124.8 3.9 %shard_map.115 = bf16[4,1600,128]{2,1,0:T(8,128)(2,1)S(1)} custom-call(s32[4,128]{1,0:T(4,128)S(1)} %get-tuple-element.25.target_ref, bf16[64,200,128]{2,1,0:T(8,128)(2,1)} %all-to-all-done.1.back_ref), custom_call_target="tpu_custom_call" | custom-call | flops 1677721600 | bytes 6553600 | tf_op jit(solution)/shard_map/pallas_call | solution.py:229
  128.7 5.0 %copy.40 = bf16[4,40,40,128]{1,2,3,0:T(8,128)(2,1)} copy(bf16[4,40,40,128]{3,2,1,0:T(8,128)(2,1)S(1)} %bitcast.55) | data formatting | bytes 3276800 | tf_op jit(solution)/shard_map/reshape | solution.py:229
  133.7 10.9 %multiply_reduce_fusion.1 = f32[128,40,40]{2,1,0:T(8,128)} fusion(f32[4,128]{1,0:T(4,128)S(1)} %copy-done.6, bf16[40,40,4,128]{1,0,3,2:T(8,128)(2,1)} %copy.41, bf16[4,40,40,128]{1,2,3,0:T(8,128)(2,1)} %copy.40), kind=kOutput, calls=%fused_computation.3 | convolution fusion | flops 133324800 | bytes 4098048 | tf_op jit(solution)/shard_map/adcp,edcp->aecp/dot_general | solution.py:238
  144.6 2.8 copy.44
  149.2 2.2 collective-permute-start.12
  151.4 2.6 collective-permute-done.11.low_there
  154.0 2.5 collective-permute-done.12.high_there
  156.6 2.3 collective-permute-start.13
  159.2 4.5 %collective-permute-done.13.low_there = bf16[800,128]{1,0:T(8,128)(2,1)S(1)} collective-permute-done((bf16[800,128]{1,0:T(8,128)(2,1)S(1)}, bf16[800,128]{1,0:T(8,128)(2,1)S(1)}, u32[]{:S(2)}, u32[]{:S(2)}) %collective-permute-start.13) | collective-permute-done | bytes 204832 | tf_op jit(solution)/shard_map/ppermute | solution.py:251
  164.9 2.2 shard_map.122
  167.1 83.9 %all_to_all.21.back_ref = bf16[64,200,128]{2,1,0:T(8,128)(2,1)S(1)} all-to-all(bf16[64,200,128]{2,1,0:T(8,128)(2,1)S(1)} %shard_map.122), channel_id=1, replica_groups=mesh['row'=8,'col'=8,'fit'=4] {'row','col'}, dimensions={0} | all-to-all | bytes 6553600 | tf_op jit(solution)/shard_map/all_to_all | solution.py:226
  251.0 2.1 shard_map.123
  253.0 5.0 %copy.49 = bf16[4,40,40,128]{1,2,3,0:T(8,128)(2,1)} copy(bf16[4,40,40,128]{3,2,1,0:T(8,128)(2,1)S(1)} %bitcast.54) | data formatting | bytes 3276800 | tf_op jit(solution)/shard_map/reshape | solution.py:229
  258.0 10.9 %multiply_reduce_fusion = f32[128,40,40]{2,1,0:T(8,128)} fusion(f32[4,128]{1,0:T(4,128)S(1)} %copy-done.6, bf16[40,40,4,128]{1,0,3,2:T(8,128)(2,1)} %copy.41, bf16[4,40,40,128]{1,2,3,0:T(8,128)(2,1)} %copy.49), kind=kOutput, calls=%fused_computation.2 | convolution fusion | flops 133324800 | bytes 4098048 | tf_op jit(solution)/shard_map/adcp,edcp->aecp/dot_general | solution.py:238
  268.9 2.8 copy.53
  273.4 4.8 %collective-permute-done.15.low_there = bf16[800,128]{1,0:T(8,128)(2,1)S(1)} collective-permute-done((bf16[800,128]{1,0:T(8,128)(2,1)S(1)}, bf16[800,128]{1,0:T(8,128)(2,1)S(1)}, u32[]{:S(2)}, u32[]{:S(2)}) %collective-permute-start.15) | collective-permute-done | bytes 204832 | tf_op jit(solution)/shard_map/ppermute | solution.py:251
  281.3 5.5 %collective-permute-done.17.low_there = bf16[800,128]{1,0:T(8,128)(2,1)S(1)} collective-permute-done((bf16[800,128]{1,0:T(8,128)(2,1)S(1)}, bf16[800,128]{1,0:T(8,128)(2,1)S(1)}, u32[]{:S(2)}, u32[]{:S(2)}) %collective-permute-start.17) | collective-permute-done | bytes 204832 | tf_op jit(solution)/shard_map/ppermute | solution.py:251
  288.0 2.3 divide_subtract_fusion
  (69 shorter events, 23.6 us)
Async XLA Ops:
  0.6 26.0 %collective-permute-start = (bf16[2,40,640]{2,1,0:T(8,128)(2,1)}, bf16[2,40,640]{2,1,0:T(8,128)(2,1)S(1)}, u32[]{:S(2)}, u32[]{:S(2)}) collective-permute-start(bf16[2,40,640]{2,1,0:T(8,128)(2,1)} %refs_0_.1), channel_id=1, source_target_pairs={{0,4},{4,8},{8,12},{12,16},{16,20},{20,24},{24,28},{28,0},{1,5},{5... | collective-permute-start | bytes 307208 | tf_op jit(solution)/shard_map/ppermute | solution.py:161
  2.6 26.8 %collective-permute-start.1 = (bf16[2,40,640]{2,1,0:T(8,128)(2,1)}, bf16[2,40,640]{2,1,0:T(8,128)(2,1)S(1)}, u32[]{:S(2)}, u32[]{:S(2)}) collective-permute-start(bf16[2,40,640]{2,1,0:T(8,128)(2,1)} %refs_0_.1), channel_id=1, source_target_pairs={{0,8},{4,12},{8,16},{12,20},{16,24},{20,28},{24,0},{28,4},{1,9},{5... | collective-permute-start | bytes 307208 | tf_op jit(solution)/shard_map/ppermute | solution.py:161
  7.1 23.8 %collective-permute-start.2 = (bf16[2,40,640]{2,1,0:T(8,128)(2,1)}, bf16[2,40,640]{2,1,0:T(8,128)(2,1)S(1)}, u32[]{:S(2)}, u32[]{:S(2)}) collective-permute-start(bf16[2,40,640]{2,1,0:T(8,128)(2,1)} %refs_0_.1), channel_id=1, source_target_pairs={{0,12},{4,16},{8,20},{12,24},{16,28},{20,0},{24,4},{28,8},{1,13},{... | collective-permute-start | bytes 307208 | tf_op jit(solution)/shard_map/ppermute | solution.py:161
  9.0 23.4 %collective-permute-start.3 = (bf16[2,40,640]{2,1,0:T(8,128)(2,1)}, bf16[2,40,640]{2,1,0:T(8,128)(2,1)S(1)}, u32[]{:S(2)}, u32[]{:S(2)}) collective-permute-start(bf16[2,40,640]{2,1,0:T(8,128)(2,1)} %refs_0_.1), channel_id=1, source_target_pairs={{0,16},{4,20},{8,24},{12,28},{16,0},{20,4},{24,8},{28,12},{1,17},{... | collective-permute-start | bytes 307208 | tf_op jit(solution)/shard_map/ppermute | solution.py:161
  10.5 24.8 %collective-permute-start.4 = (bf16[2,40,640]{2,1,0:T(8,128)(2,1)}, bf16[2,40,640]{2,1,0:T(8,128)(2,1)S(1)}, u32[]{:S(2)}, u32[]{:S(2)}) collective-permute-start(bf16[2,40,640]{2,1,0:T(8,128)(2,1)} %refs_0_.1), channel_id=1, source_target_pairs={{0,20},{4,24},{8,28},{12,0},{16,4},{20,8},{24,12},{28,16},{1,21},{... | collective-permute-start | bytes 307208 | tf_op jit(solution)/shard_map/ppermute | solution.py:161
  13.6 0.7 copy-start.1
  14.3 0.7 copy-start.2
  15.0 0.7 copy-start.3
  17.3 20.6 %all-to-all-start = ((f32[64,1,128]{2,1,0:T(1,128)}), f32[64,1,128]{2,1,0:T(1,128)S(1)}, u32[]{:S(2)}, u32[]{:S(2)}) async-start(f32[64,1,128]{2,1,0:T(1,128)} %bitcast.5), calls=%async_computation | async-start | bytes 65536 | tf_op jit(solution)/shard_map/all_to_all | solution.py:207
  26.7 15.1 %collective-permute-start.5 = (bf16[2,40,640]{2,1,0:T(8,128)(2,1)}, bf16[2,40,640]{2,1,0:T(8,128)(2,1)S(1)}, u32[]{:S(2)}, u32[]{:S(2)}) collective-permute-start(bf16[2,40,640]{2,1,0:T(8,128)(2,1)} %refs_0_.1), channel_id=1, source_target_pairs={{0,24},{4,28},{8,0},{12,4},{16,8},{20,12},{24,16},{28,20},{1,25},{... | collective-permute-start | bytes 307208 | tf_op jit(solution)/shard_map/ppermute | solution.py:161
  29.4 12.3 %collective-permute-start.6 = (bf16[2,40,640]{2,1,0:T(8,128)(2,1)}, bf16[2,40,640]{2,1,0:T(8,128)(2,1)S(1)}, u32[]{:S(2)}, u32[]{:S(2)}) collective-permute-start(bf16[2,40,640]{2,1,0:T(8,128)(2,1)} %refs_0_.1), channel_id=1, source_target_pairs={{0,28},{4,0},{8,4},{12,8},{16,12},{20,16},{24,20},{28,24},{1,29},{... | collective-permute-start | bytes 307208 | tf_op jit(solution)/shard_map/ppermute | solution.py:161
  30.9 10.9 %collective-permute-start.7 = (bf16[2,40,640]{2,1,0:T(8,128)(2,1)}, bf16[2,40,640]{2,1,0:T(8,128)(2,1)S(1)}, u32[]{:S(2)}, u32[]{:S(2)}) collective-permute-start(bf16[2,40,640]{2,1,0:T(8,128)(2,1)} %refs_0_.1), channel_id=1, source_target_pairs={{0,64},{32,96},{64,128},{96,160},{128,192},{160,224},{192,0},{224,... | collective-permute-start | bytes 307208 | tf_op jit(solution)/shard_map/ppermute | solution.py:161
  32.4 9.4 %collective-permute-start.8 = (bf16[2,40,640]{2,1,0:T(8,128)(2,1)}, bf16[2,40,640]{2,1,0:T(8,128)(2,1)S(1)}, u32[]{:S(2)}, u32[]{:S(2)}) collective-permute-start(bf16[2,40,640]{2,1,0:T(8,128)(2,1)} %refs_0_.1), channel_id=1, source_target_pairs={{0,128},{32,160},{64,192},{96,224},{128,0},{160,32},{192,64},{224,... | collective-permute-start | bytes 307208 | tf_op jit(solution)/shard_map/ppermute | solution.py:161
  35.3 6.5 %collective-permute-start.9 = (bf16[2,40,640]{2,1,0:T(8,128)(2,1)}, bf16[2,40,640]{2,1,0:T(8,128)(2,1)S(1)}, u32[]{:S(2)}, u32[]{:S(2)}) collective-permute-start(bf16[2,40,640]{2,1,0:T(8,128)(2,1)} %refs_0_.1), channel_id=1, source_target_pairs={{0,192},{32,224},{64,0},{96,32},{128,64},{160,96},{192,128},{224,1... | collective-permute-start | bytes 307208 | tf_op jit(solution)/shard_map/ppermute | solution.py:161
  37.8 10.4 %copy-start.7 = (s32[128]{0:T(128)S(1)}, s32[128]{0:T(128)}, u32[]{:S(2)}) copy-start(s32[128]{0:T(128)} %param.13) | copy-start | bytes 1540
  37.8 10.5 %copy-start.8 = (s32[128]{0:T(128)S(1)}, s32[128]{0:T(128)}, u32[]{:S(2)}) copy-start(s32[128]{0:T(128)} %param.12) | copy-start | bytes 1540
  37.9 10.5 %copy-start = (bf16[2,40,640]{2,1,0:T(8,128)(2,1)S(1)}, bf16[2,40,640]{2,1,0:T(8,128)(2,1)}, u32[]{:S(2)}) copy-start(bf16[2,40,640]{2,1,0:T(8,128)(2,1)} %refs_0_.1) | copy-start | bytes 307204
  41.8 83.0 %all-to-all-start.1 = ((bf16[64,200,128]{2,1,0:T(8,128)(2,1)}), bf16[64,200,128]{2,1,0:T(8,128)(2,1)}, u32[]{:S(2)}, u32[]{:S(2)}) async-start(bf16[64,200,128]{2,1,0:T(8,128)(2,1)} %shard_map.114), calls=%async_computation.1 | async-start | bytes 6553600 | tf_op jit(solution)/shard_map/all_to_all | solution.py:226
  48.2 7.1 %copy-start.5 = (f32[40,128]{1,0:T(8,128)S(1)}, f32[40,128]{1,0:T(8,128)}, u32[]{:S(2)}) copy-start(f32[40,128]{1,0:T(8,128)} %param.14) | copy-start | bytes 61444
  48.4 12.2 %collective-permute-start.10 = (bf16[8,40,640]{2,1,0:T(8,128)(2,1)S(1)}, bf16[8,40,640]{2,1,0:T(8,128)(2,1)S(1)}, u32[]{:S(2)}, u32[]{:S(2)}) collective-permute-start(bf16[8,40,640]{2,1,0:T(8,128)(2,1)S(1)} %shard_map.116.refs_0_), channel_id=1, source_target_pairs={{0,32},{32,0},{64,96},{96,64},{128,160},{160,128},{192,224},{224,1... | collective-permute-start | bytes 1228808 | tf_op jit(solution)/shard_map/ppermute | solution.py:174
  124.8 9.0 %copy-start.6 = (f32[4,128]{1,0:T(4,128)S(1)}, f32[4,128]{1,0:T(4,128)}, u32[]{:S(2)}) copy-start(f32[4,128]{1,0:T(4,128)} %param.17) | copy-start | bytes 6148
  144.6 20.1 %copy-start.4 = (f32[40,40,128]{2,1,0:T(8,128)S(1)}, f32[40,40,128]{2,1,0:T(8,128)}, u32[]{:S(2)}) copy-start(f32[40,40,128]{2,1,0:T(8,128)} %broadcast_add_fusion) | copy-start | bytes 2457604
  147.5 6.5 %collective-permute-start.11 = (bf16[800,128]{1,0:T(8,128)(2,1)S(1)}, bf16[800,128]{1,0:T(8,128)(2,1)S(1)}, u32[]{:S(2)}, u32[]{:S(2)}) collective-permute-start(bf16[800,128]{1,0:T(8,128)(2,1)S(1)} %get-tuple-element.40.low_ref), channel_id=1, source_target_pairs={{0,1},{1,0},{2,3},{3,2},{4,5},{5,4},{6,7},{7,6},{8,9},{9,8},{10,11... | collective-permute-start | bytes 614408 | tf_op jit(solution)/shard_map/ppermute | solution.py:251
  149.2 7.3 %collective-permute-start.12 = (bf16[800,128]{1,0:T(8,128)(2,1)S(1)}, bf16[800,128]{1,0:T(8,128)(2,1)S(1)}, u32[]{:S(2)}, u32[]{:S(2)}) collective-permute-start(bf16[800,128]{1,0:T(8,128)(2,1)S(1)} %get-tuple-element.41.high_ref), channel_id=1, source_target_pairs={{0,3},{1,2},{2,1},{3,0},{4,7},{5,6},{6,5},{7,4},{8,11},{9,10},{10,... | collective-permute-start | bytes 614408 | tf_op jit(solution)/shard_map/ppermute | solution.py:251
  156.6 7.1 %collective-permute-start.13 = (bf16[800,128]{1,0:T(8,128)(2,1)S(1)}, bf16[800,128]{1,0:T(8,128)(2,1)S(1)}, u32[]{:S(2)}, u32[]{:S(2)}) collective-permute-start(bf16[800,128]{1,0:T(8,128)(2,1)S(1)} %get-tuple-element.42.low_ref), channel_id=1, source_target_pairs={{0,3},{1,2},{2,1},{3,0},{4,7},{5,6},{6,5},{7,4},{8,11},{9,10},{10,... | collective-permute-start | bytes 614408 | tf_op jit(solution)/shard_map/ppermute | solution.py:251
  158.9 5.8 %collective-permute-start.14 = (bf16[800,128]{1,0:T(8,128)(2,1)S(1)}, bf16[800,128]{1,0:T(8,128)(2,1)S(1)}, u32[]{:S(2)}, u32[]{:S(2)}) collective-permute-start(bf16[800,128]{1,0:T(8,128)(2,1)S(1)} %get-tuple-element.43.high_ref), channel_id=1, source_target_pairs={{0,1},{1,0},{2,3},{3,2},{4,5},{5,4},{6,7},{7,6},{8,9},{9,8},{10,11... | collective-permute-start | bytes 614408 | tf_op jit(solution)/shard_map/ppermute | solution.py:251
  271.8 6.5 %collective-permute-start.15 = (bf16[800,128]{1,0:T(8,128)(2,1)S(1)}, bf16[800,128]{1,0:T(8,128)(2,1)S(1)}, u32[]{:S(2)}, u32[]{:S(2)}) collective-permute-start(bf16[800,128]{1,0:T(8,128)(2,1)S(1)} %get-tuple-element.44.low_ref), channel_id=1, source_target_pairs={{0,1},{1,0},{2,3},{3,2},{4,5},{5,4},{6,7},{7,6},{8,9},{9,8},{10,11... | collective-permute-start | bytes 614408 | tf_op jit(solution)/shard_map/ppermute | solution.py:251
  272.1 7.5 %collective-permute-start.16 = (bf16[800,128]{1,0:T(8,128)(2,1)S(1)}, bf16[800,128]{1,0:T(8,128)(2,1)S(1)}, u32[]{:S(2)}, u32[]{:S(2)}) collective-permute-start(bf16[800,128]{1,0:T(8,128)(2,1)S(1)} %get-tuple-element.45.high_ref), channel_id=1, source_target_pairs={{0,3},{1,2},{2,1},{3,0},{4,7},{5,6},{6,5},{7,4},{8,11},{9,10},{10,... | collective-permute-start | bytes 614408 | tf_op jit(solution)/shard_map/ppermute | solution.py:251
  279.7 7.1 %collective-permute-start.17 = (bf16[800,128]{1,0:T(8,128)(2,1)S(1)}, bf16[800,128]{1,0:T(8,128)(2,1)S(1)}, u32[]{:S(2)}, u32[]{:S(2)}) collective-permute-start(bf16[800,128]{1,0:T(8,128)(2,1)S(1)} %get-tuple-element.46.low_ref), channel_id=1, source_target_pairs={{0,3},{1,2},{2,1},{3,0},{4,7},{5,6},{6,5},{7,4},{8,11},{9,10},{10,... | collective-permute-start | bytes 614408 | tf_op jit(solution)/shard_map/ppermute | solution.py:251
  281.3 5.8 %collective-permute-start.18 = (bf16[800,128]{1,0:T(8,128)(2,1)S(1)}, bf16[800,128]{1,0:T(8,128)(2,1)S(1)}, u32[]{:S(2)}, u32[]{:S(2)}) collective-permute-start(bf16[800,128]{1,0:T(8,128)(2,1)S(1)} %get-tuple-element.47.high_ref), channel_id=1, source_target_pairs={{0,1},{1,0},{2,3},{3,2},{4,5},{5,4},{6,7},{7,6},{8,9},{9,8},{10,11... | collective-permute-start | bytes 614408 | tf_op jit(solution)/shard_map/ppermute | solution.py:251
